TPU v7x, 256 devices: a whole 4x4x8 slice. The times are simulated.
256 devices in a mesh: rep: 128 (over x, z, y_hi, core), dom: 2 (over y_lo).
Axes of the slice: x: 4, y: 4 (y_hi: 2, y_lo: 2; y = y_hi * 2 + y_lo), z: 8, core: 2. Of those that a mesh axis runs over, the one named last changes fastest.
Arguments:
- field: float32 [128, 256, 2048], P('rep', 'dom'), may hold values from -2.5 to 2.5
- momentum: float32 [128, 256, 2048], P('rep', 'dom'), may hold values from -4 to 4
- labels: int32 [128], P('rep'), may hold values from 0 to 127, each once
- betas: float32 [128], replicated, may hold values from 0.4 to 1.6
- accept: int32 [128], P('rep'), may hold values 0 or 1
- swap_pairs: int32 [128], replicated, may hold values from 0 to 127, as said below
Outputs:
- field_out: float32 [128, 256, 2048], P('rep', 'dom')
- field_sorted: float32 [128, 256, 2048], P('rep', 'dom')
- labels_out: int32 [128], P('rep')
- energy_change: float32 [128], P('rep')
- ladder_action: float32 [128], P('rep')
Inputs may be any that keep to these rules, and one draw needn't show every extreme that they name: Each temperature index t is paired with itself, with t - 1 or with t + 1, and the pairing is symmetric: swap_pairs[swap_pairs[t]] = t. labels is a permutation of the temperature indices.
All inputs are finite; a program needn't handle non-finite values. No bound on the sum of `accept` on one device may be relied on, other than what follows from the above.
Results may differ from a plain program's by a relative error of at most 0.0003.
Values sent between devices are 32-bit elements; how exact they have to be, the bound alone decides.
A program may use at most 64 MiB of HBM per device.

v0:
```python
import jax
import jax.numpy as jnp
from jax import lax
from jax.sharding import Mesh
from jax.sharding import PartitionSpec as P

STEPS = 8
REP = ("rep_0", "rep_1", "rep_2", "rep_3")


hopping = 0.18
quartic = 0.3
step_size = 0.05


def with_halo(cells, sides, width):
    for axis, dim in sides:
        count = lax.axis_size(axis)
        head = lax.slice_in_dim(cells, 0, width, axis=dim)
        tail = lax.slice_in_dim(cells, cells.shape[dim] - width, cells.shape[dim], axis=dim)
        cells = jnp.concatenate(
            [
                lax.ppermute(tail, axis, [(i, (i + 1) % count) for i in range(count)]),
                cells,
                lax.ppermute(head, axis, [((i + 1) % count, i) for i in range(count)]),
            ],
            axis=dim,
        )
    return cells


def from_everyone(shard, axis):
    peers = lax.axis_size(axis)
    return lax.all_to_all(
        jnp.broadcast_to(shard[None], (peers, *shard.shape)), axis, 0, 0, tiled=True
    )


def taken_together(shard, axis):
    return from_everyone(shard, axis).sum(axis=0)


def in_one(arrays, axis):
    ravelled, at, gathered = (jnp.concatenate([a.reshape(-1) for a in arrays]), 0, [])
    subtotal = taken_together(ravelled, axis)
    for a in arrays:
        gathered.append(subtotal[at : at + a.size].reshape(a.shape))
        at += a.size
    return tuple(gathered)


def cut_along(shard, dim, peers):
    dims = shard.shape
    tiles = shard.reshape(*dims[:dim], peers, dims[dim] // peers, *dims[dim + 1 :])
    return jnp.moveaxis(tiles, dim, 0)


def laid_out(tiles, dim):
    tiles = jnp.moveaxis(tiles, 0, dim)
    dims = tiles.shape
    return tiles.reshape(*dims[:dim], dims[dim] * dims[dim + 1], *dims[dim + 2 :])


def exchange_in_order(tiles, axes, order):
    dims = [lax.axis_size(a) for a in axes]
    tiles = tiles.reshape(*dims, *tiles.shape[1:])
    for k in order:
        tiles = lax.all_to_all(tiles, axes[k], split_axis=k, concat_axis=k, tiled=True)
    return tiles.reshape(-1, *tiles.shape[len(axes) :])


def two_step_exchange(shard, groups, order, split_dim, concat_dim):
    peers = lax.axis_size(groups[0]) * lax.axis_size(groups[1])
    tiles = cut_along(shard, split_dim, peers)
    return laid_out(exchange_in_order(tiles, groups, order), concat_dim)


def force_rows(padded, coldness):
    centre = padded[1:-1]
    beside_all = padded[:-2] + padded[2:] + (jnp.roll(centre, 1, 1) + jnp.roll(centre, -1, 1))
    return coldness * (
        -2.0 * hopping * beside_all
        + 2.0 * centre
        + 4.0 * quartic * centre * (centre * centre - 1.0)
    )


def site_terms(padded, margin, strip_rows):
    values = padded[margin : margin + strip_rows]
    lower_row = padded[margin + 1 : margin + 1 + strip_rows]
    neighbours = lower_row + jnp.roll(values, -1, 1)
    squared = values * values
    return (
        -2.0 * hopping * values * neighbours + squared + quartic * (squared - 1.0) * (squared - 1.0)
    )


def trim_rows(values, margin, target):
    excess = margin - target
    return values[excess : values.shape[0] - excess]


def info_rows(label_value, action, members, lanes):
    pair = jnp.concatenate((label_value[None], action))
    front = jnp.broadcast_to(pair[None, None, :], (members, 1, 2))
    return jnp.concatenate((front, jnp.zeros((members, 1, lanes - 2), jnp.float32)), 2)


def body(field, momentum, labels, betas, accept, swap_pairs):
    strip_rows = field.shape[1]
    width = field.shape[2]
    ladder_index = jnp.arange(betas.shape[0], dtype=jnp.int32)
    chosen = ladder_index == labels[0]
    coldness = jnp.sum(jnp.where(chosen, betas, 0.0))
    new_label = jnp.sum(jnp.where(chosen, swap_pairs, 0))
    start_field = field[0]
    start_moment = momentum[0]
    current = start_field
    moment = start_moment
    margin = 0
    old_action = None
    new_action = None
    for leap_step in range(STEPS + 1):
        if margin == 0:
            stacked = with_halo(jnp.stack((current, moment)), (("dom", 1),), 3)
            current = stacked[0]
            moment = stacked[1]
            margin = 3
        padded = current
        outer = margin
        if leap_step == 0:
            old_action = site_terms(padded, outer, strip_rows)
        if leap_step == STEPS:
            new_action = site_terms(padded, outer, strip_rows)
        force_now = force_rows(padded, coldness)
        moment = trim_rows(moment, margin, outer - 1)
        current = trim_rows(padded, outer, outer - 1)
        margin = outer - 1
        factor = 0.5 * step_size if leap_step == 0 or leap_step == STEPS else step_size
        moment = moment - factor * force_now
        if leap_step < STEPS:
            current = current + step_size * moment
    change_part = jnp.sum(
        0.5 * moment * moment
        + coldness * new_action
        - (0.5 * start_moment * start_moment + coldness * old_action)
    )
    accepted = accept[0] == 1
    action_part = jnp.where(accepted, jnp.sum(new_action), jnp.sum(old_action))
    field_out = jnp.where(accepted, current, start_field)
    label_value = new_label.astype(jnp.float32)
    change, action = in_one((change_part[None], action_part[None]), "dom")
    members = lax.axis_size(REP)
    lanes = 128
    blocks = field_out.reshape(members, -1, 128)
    outgoing = jnp.concatenate((blocks, info_rows(label_value, action, members, lanes)), 1)
    spread = two_step_exchange(outgoing, (("rep_0", "rep_1", "rep_2"), "rep_3"), (1, 0), 0, 0)
    label_values = spread[:, -1, 0]
    actions = spread[:, -1, 1]
    received = spread[:, :-1]
    held_labels = label_values.astype(jnp.int32)
    onehot = held_labels[None, :] == ladder_index[:, None]
    holder = jnp.sum(jnp.where(onehot, ladder_index[None, :], 0), 1)
    sites_total = lax.axis_size("dom") * strip_rows * width
    ladder_all = jnp.sum(jnp.where(onehot, actions[None, :], 0.0), 1) / sites_total
    ladder = lax.dynamic_slice_in_dim(ladder_all, lax.axis_index(REP), 1)
    ordered = jnp.take(received, holder, axis=0)
    gathered = lax.all_to_all(ordered, REP, split_axis=0, concat_axis=0, tiled=True)
    returned = gathered.reshape(1, strip_rows, width)
    return (field_out[None], returned, new_label[None], change, ladder)


def solution(mesh):
    torus = Mesh(
        mesh.devices.reshape(4, 8, 2, 2, mesh.shape["dom"]),
        ("rep_0", "rep_1", "rep_2", "rep_3", "dom"),
    )
    in_specs = (P(REP, "dom", None), P(REP, "dom", None), P(REP), P(), P(REP), P())
    out_specs = (P(REP, "dom", None), P(REP, "dom", None), P(REP), P(REP), P(REP))
    return jax.shard_map(body, mesh=torus, in_specs=in_specs, out_specs=out_specs, check_vma=False)
```

profile of v0, /device:TPU:1, one launch (start us, length us, event | category | flops | bytes accessed | tf_op | source)
XLA Modules:
  0.0 151.5 jit_solution(8558482204388638383)
XLA Ops:
  0.6 1.4 constant_dynamic-update-slice_fusion.1
  2.3 2.2 %collective-permute-start.1 = (f32[2,3,2048]{2,1,0:T(4,128)S(1)}, f32[2,3,2048]{2,1,0:T(4,128)S(1)}, u32[]{:S(2)}, u32[]{:S(2)}) collective-permute-start(f32[2,3,2048]{2,1,0:T(4,128)S(1)} %get-tuple-element.31), channel_id=1, source_target_pairs={{1,0},{0,1},{3,2},{2,3},{5,4},{4,5},{7,6},{6,7},{9,8},{8,9},{11,10... | collective-permute-start | bytes 147464 | tf_op jit(solution)/shard_map/ppermute | solution.py:25
  6.2 1.5 collective-permute-done
  8.5 1.5 %multiply_add_fusion.5 = (f32[132,2048]{1,0:T(8,128)S(1)}, f32[132,2048]{1,0:T(8,128)S(1)}) fusion(f32[2,134,2048]{2,1,0:T(8,128)S(1)} %pad_maximum_fusion, f32[132,1]{1,0:T(8,128)S(1)} %get-tuple-element.68, f32[132,2047]{1,0:T(8,128)S(1)} %get-tuple-element.70, f32[132,2047]{1,0:T(8,128)S(1)} %get-tuple-element.69, f32[132,1]{1,0:T(8,128)S(1)} %get-tuple-element.67, ...), kind=kLoop, calls=%fused_computation.77 | loop fusion | flops 4866048 | bytes 8650756 | tf_op jit(solution)/shard_map/add | solution.py:142
  10.6 1.5 %multiply_add_fusion.4 = (f32[130,2048]{1,0:T(8,128)S(1)}, f32[130,2048]{1,0:T(8,128)S(1)}) fusion(f32[132,2048]{1,0:T(8,128)S(1)} %get-tuple-element.22, f32[130,1]{1,0:T(8,128)S(1)} %get-tuple-element.64, f32[130,2047]{1,0:T(8,128)S(1)} %get-tuple-element.66, f32[130,2047]{1,0:T(8,128)S(1)} %get-tuple-element.65, f32[130,1]{1,0:T(8,128)S(1)} %get-tuple-element.63, ...), kind=kLoop, calls=%fused_computation.76 | loop fusion | flops 4792320 | bytes 8519684 | tf_op jit(solution)/shard_map/add | solution.py:142
  12.6 1.5 add_bitcast_fusion.1
  14.1 1.2 collective-permute-start.2
  15.7 1.6 %collective-permute-done.2 = f32[2,3,2048]{2,1,0:T(4,128)S(1)} collective-permute-done((f32[2,3,2048]{2,1,0:T(4,128)S(1)}, f32[2,3,2048]{2,1,0:T(4,128)S(1)}, u32[]{:S(2)}, u32[]{:S(2)}) %collective-permute-start.2) | collective-permute-done | bytes 49184 | tf_op jit(solution)/shard_map/ppermute | solution.py:23
  17.3 1.1 collective-permute-done.3
  19.4 1.5 %multiply_add_fusion.3 = (f32[132,2048]{1,0:T(8,128)S(1)}, f32[132,2048]{1,0:T(8,128)S(1)}) fusion(f32[2,134,2048]{2,1,0:T(8,128)S(1)} %pad_maximum_fusion.1, f32[132,1]{1,0:T(8,128)S(1)} %get-tuple-element.56, f32[132,2047]{1,0:T(8,128)S(1)} %get-tuple-element.58, f32[132,2047]{1,0:T(8,128)S(1)} %get-tuple-element.57, f32[132,1]{1,0:T(8,128)S(1)} %get-tuple-element.55, ...), kind=kLoop, calls=%fused_computation.75 | loop fusion | flops 4866048 | bytes 8650756 | tf_op jit(solution)/shard_map/add | solution.py:142
  21.4 1.5 %multiply_add_fusion.2 = (f32[130,2048]{1,0:T(8,128)S(1)}, f32[130,2048]{1,0:T(8,128)S(1)}) fusion(f32[132,2048]{1,0:T(8,128)S(1)} %get-tuple-element.16, f32[130,1]{1,0:T(8,128)S(1)} %get-tuple-element.52, f32[130,2047]{1,0:T(8,128)S(1)} %get-tuple-element.54, f32[130,2047]{1,0:T(8,128)S(1)} %get-tuple-element.53, f32[130,1]{1,0:T(8,128)S(1)} %get-tuple-element.51, ...), kind=kLoop, calls=%fused_computation.74 | loop fusion | flops 4792320 | bytes 8519684 | tf_op jit(solution)/shard_map/add | solution.py:142
  23.4 1.5 add_bitcast_fusion
  25.0 0.9 copy-done.1
  26.9 0.8 collective-permute-start.5
  28.3 1.3 slice.527
  31.0 1.9 %pad_maximum_fusion.2 = f32[2,134,2048]{2,1,0:T(8,128)S(1)} fusion(f32[2,3,2048]{2,1,0:T(4,128)S(1)} %collective-permute-done.5, f32[1,128,2048]{2,1,0:T(8,128)} %bitcast.137, f32[1,128,2048]{2,1,0:T(8,128)} %copy-done.1, f32[2,3,2048]{2,1,0:T(4,128)S(1)} %collective-permute-done.4), kind=kLoop, calls=%fused_computation.3 | loop fusion | flops 1646592 | bytes 4390912 | tf_op jit(solution)/shard_map/concatenate | solution.py:21
  33.4 1.5 %multiply_add_fusion.1 = (f32[132,2048]{1,0:T(8,128)S(1)}, f32[132,2048]{1,0:T(8,128)S(1)}) fusion(f32[2,134,2048]{2,1,0:T(8,128)S(1)} %pad_maximum_fusion.2, f32[132,1]{1,0:T(8,128)S(1)} %get-tuple-element.44, f32[132,2047]{1,0:T(8,128)S(1)} %get-tuple-element.46, f32[132,2047]{1,0:T(8,128)S(1)} %get-tuple-element.45, f32[132,1]{1,0:T(8,128)S(1)} %get-tuple-element.43, ...), kind=kLoop, calls=%fused_computation.73 | loop fusion | flops 4866048 | bytes 8650756 | tf_op jit(solution)/shard_map/add | solution.py:142
  35.5 1.5 %multiply_add_fusion = (f32[130,2048]{1,0:T(8,128)S(1)}, f32[130,2048]{1,0:T(8,128)S(1)}) fusion(f32[132,2048]{1,0:T(8,128)S(1)} %get-tuple-element.10, f32[130,1]{1,0:T(8,128)S(1)} %get-tuple-element.40, f32[130,2047]{1,0:T(8,128)S(1)} %get-tuple-element.42, f32[130,2047]{1,0:T(8,128)S(1)} %get-tuple-element.41, f32[130,1]{1,0:T(8,128)S(1)} %get-tuple-element.39, ...), kind=kLoop, calls=%fused_computation.72 | loop fusion | flops 4792320 | bytes 8519684 | tf_op jit(solution)/shard_map/add | solution.py:142
  37.5 0.7 copy-done.4
  38.6 4.6 %fusion.76 = (f32[16,8,16,128]{3,1,2,0:T(8,128)S(1)}, f32[1,128,2048]{2,1,0:T(8,128)}, f32[]{:T(128)}, f32[]{:T(128)}, f32[]{:T(128)}) fusion(f32[130,2048]{1,0:T(8,128)S(1)} %get-tuple-element.8, pred[]{:T(512)} %bitcast, f32[1,128,2048]{2,1,0:T(8,128)S(1)} %copy-done, f32[1,128,2048]{2,1,0:T(8,128)S(1)} %copy-done.4, f32[128,1]{1,0:T(8,128)S(1)} %get-tuple-element.37, ...), kind=kLoop, calls=%fused_computation.121 | loop fusion | flops 12320765 | bytes 13680657
  44.5 0.8 pad_maximum_fusion.10
  45.3 4.9 %all_to_all.21 = f32[2,1,2]{2,1,0:T(1,128)S(1)} all-to-all(f32[2,1,2]{2,1,0:T(1,128)S(1)} %broadcast_in_dim.81), channel_id=1, replica_groups=mesh['rep_0'=4,'rep_1'=8,'rep_2'=2,'rep_3'=2,'dom'=2] {'dom'}, dimensions={0} | all-to-all | bytes 32 | tf_op jit(solution)/shard_map/all_to_all | solution.py:34
  50.9 0.7 fusion.81
  52.1 10.2 %all_to_all.22 = f32[64,2,1,17,128]{4,0,3,2,1:T(8,128)S(1)} all-to-all(f32[64,2,1,17,128]{4,0,3,2,1:T(8,128)S(1)} %copy.29), channel_id=1, replica_groups=mesh['rep_0'=4,'rep_1'=8,'rep_2'=2,'rep_3'=2,'dom'=2] {'rep_3'}, dimensions={1} | all-to-all | bytes 2228224 | tf_op jit(solution)/shard_map/all_to_all | solution.py:68
  62.4 0.9 copy.30
  63.2 43.0 %all_to_all.23 = f32[64,2,1,17,128]{4,1,3,2,0:T(2,128)S(1)} all-to-all(f32[64,2,1,17,128]{4,1,3,2,0:T(2,128)S(1)} %copy.30), channel_id=1, replica_groups=mesh['rep_0'=4,'rep_1'=8,'rep_2'=2,'rep_3'=2,'dom'=2] {'rep_0','rep_1','..., dimensions={0} | all-to-all | bytes 2228224 | tf_op jit(solution)/shard_map/all_to_all | solution.py:68
  107.2 1.6 %copy.33 = f32[128,16,128]{2,1,0:T(8,128)} copy(f32[128,16,128]{2,0,1:T(8,128)S(1)} %slice.530) | data formatting | bytes 2097152
  108.8 1.9 %gather_fusion = f32[128,16,128]{2,1,0:T(8,128)S(1)} fusion(f32[128,16,128]{2,1,0:T(8,128)} %copy.33, s32[1024]{0:T(1024)S(1)} %pad_clamp_fusion), kind=kCustom, calls=%fused_computation | custom fusion | bytes 2097664 | tf_op jit(solution)/shard_map/jit(_take)/gather | solution.py:167
  110.6 1.2 broadcast_select_fusion
  111.8 8.7 %all-to-all-start.3 = ((f32[128,16,128]{2,1,0:T(8,128)}), f32[128,16,128]{2,1,0:T(8,128)S(1)}, u32[]{:S(2)}, u32[]{:S(2)}) async-start(f32[128,16,128]{2,1,0:T(8,128)} %broadcast_select_fusion), calls=%async_computation.3 | async-start | bytes 2097152 | tf_op jit(solution)/shard_map/all_to_all | solution.py:168
  121.4 28.9 %all-to-all-done.3 = f32[128,16,128]{2,1,0:T(8,128)S(1)} async-done(((f32[128,16,128]{2,1,0:T(8,128)}), f32[128,16,128]{2,1,0:T(8,128)S(1)}, u32[]{:S(2)}, u32[]{:S(2)}) %all-to-all-start.3) | async-done | bytes 1048608 | tf_op jit(solution)/shard_map/all_to_all | solution.py:168
  150.3 1.1 reshape.70
  (68 shorter events, 12.0 us)
Async XLA Ops:
  0.6 1.5 %copy-start.3 = (f32[1,128,2048]{2,1,0:T(8,128)S(1)}, f32[1,128,2048]{2,1,0:T(8,128)}, u32[]{:S(2)}) copy-start(f32[1,128,2048]{2,1,0:T(8,128)} %param.7) | copy-start | bytes 3145732
  2.2 3.1 %copy-start.6 = (f32[128]{0:T(128)S(1)}, f32[128]{0:T(128)}, u32[]{:S(2)}) copy-start(f32[128]{0:T(128)} %param.9) | copy-start | bytes 1540
  2.3 3.9 %collective-permute-start.1 = (f32[2,3,2048]{2,1,0:T(4,128)S(1)}, f32[2,3,2048]{2,1,0:T(4,128)S(1)}, u32[]{:S(2)}, u32[]{:S(2)}) collective-permute-start(f32[2,3,2048]{2,1,0:T(4,128)S(1)} %get-tuple-element.31), channel_id=1, source_target_pairs={{1,0},{0,1},{3,2},{2,3},{5,4},{4,5},{7,6},{6,7},{9,8},{8,9},{11,10... | collective-permute-start | bytes 147464 | tf_op jit(solution)/shard_map/ppermute | solution.py:25
  4.5 3.1 %collective-permute-start = (f32[2,3,2048]{2,1,0:T(4,128)S(1)}, f32[2,3,2048]{2,1,0:T(4,128)S(1)}, u32[]{:S(2)}, u32[]{:S(2)}) collective-permute-start(f32[2,3,2048]{2,1,0:T(4,128)S(1)} %get-tuple-element.30), channel_id=1, source_target_pairs={{0,1},{1,0},{2,3},{3,2},{4,5},{5,4},{6,7},{7,6},{8,9},{9,8},{10,11... | collective-permute-start | bytes 147464 | tf_op jit(solution)/shard_map/ppermute | solution.py:23
  14.1 3.2 %collective-permute-start.2 = (f32[2,3,2048]{2,1,0:T(4,128)S(1)}, f32[2,3,2048]{2,1,0:T(4,128)S(1)}, u32[]{:S(2)}, u32[]{:S(2)}) collective-permute-start(f32[2,3,2048]{2,1,0:T(4,128)S(1)} %get-tuple-element.28), channel_id=1, source_target_pairs={{0,1},{1,0},{2,3},{3,2},{4,5},{5,4},{6,7},{7,6},{8,9},{9,8},{10,11... | collective-permute-start | bytes 147464 | tf_op jit(solution)/shard_map/ppermute | solution.py:23
  15.3 3.1 %collective-permute-start.3 = (f32[2,3,2048]{2,1,0:T(4,128)S(1)}, f32[2,3,2048]{2,1,0:T(4,128)S(1)}, u32[]{:S(2)}, u32[]{:S(2)}) collective-permute-start(f32[2,3,2048]{2,1,0:T(4,128)S(1)} %get-tuple-element.29), channel_id=1, source_target_pairs={{1,0},{0,1},{3,2},{2,3},{5,4},{4,5},{7,6},{6,7},{9,8},{8,9},{11,10... | collective-permute-start | bytes 147464 | tf_op jit(solution)/shard_map/ppermute | solution.py:25
  24.9 1.0 copy-start.1
  24.9 1.3 copy-start.2
  24.9 2.8 %copy-start.7 = (s32[128]{0:T(128)S(1)}, s32[128]{0:T(128)}, u32[]{:S(2)}) copy-start(s32[128]{0:T(128)} %param.11) | copy-start | bytes 1540
  24.9 3.4 %copy-start = (f32[1,128,2048]{2,1,0:T(8,128)S(1)}, f32[1,128,2048]{2,1,0:T(8,128)}, u32[]{:S(2)}) copy-start(f32[1,128,2048]{2,1,0:T(8,128)} %param.6) | copy-start | bytes 3145732
  26.2 4.7 %collective-permute-start.4 = (f32[2,3,2048]{2,1,0:T(4,128)S(1)}, f32[2,3,2048]{2,1,0:T(4,128)S(1)}, u32[]{:S(2)}, u32[]{:S(2)}) collective-permute-start(f32[2,3,2048]{2,1,0:T(4,128)S(1)} %get-tuple-element.26), channel_id=1, source_target_pairs={{0,1},{1,0},{2,3},{3,2},{4,5},{5,4},{6,7},{7,6},{8,9},{9,8},{10,11... | collective-permute-start | bytes 147464 | tf_op jit(solution)/shard_map/ppermute | solution.py:23
  26.9 4.1 %collective-permute-start.5 = (f32[2,3,2048]{2,1,0:T(4,128)S(1)}, f32[2,3,2048]{2,1,0:T(4,128)S(1)}, u32[]{:S(2)}, u32[]{:S(2)}) collective-permute-start(f32[2,3,2048]{2,1,0:T(4,128)S(1)} %get-tuple-element.27), channel_id=1, source_target_pairs={{1,0},{0,1},{3,2},{2,3},{5,4},{4,5},{7,6},{6,7},{9,8},{8,9},{11,10... | collective-permute-start | bytes 147464 | tf_op jit(solution)/shard_map/ppermute | solution.py:25
  37.0 1.2 copy-start.4
  37.0 1.5 %copy-start.5 = (f32[128,2047]{1,0:T(8,128)S(1)}, f32[128,2047]{1,0:T(8,128)}, u32[]{:S(2)}) copy-start(f32[128,2047]{1,0:T(8,128)} %slice.527) | copy-start | bytes 3144196
  111.8 38.5 %all-to-all-start.3 = ((f32[128,16,128]{2,1,0:T(8,128)}), f32[128,16,128]{2,1,0:T(8,128)S(1)}, u32[]{:S(2)}, u32[]{:S(2)}) async-start(f32[128,16,128]{2,1,0:T(8,128)} %broadcast_select_fusion), calls=%async_computation.3 | async-start | bytes 2097152 | tf_op jit(solution)/shard_map/all_to_all | solution.py:168
where the time goes:
time: 152 us; the launch traced here: 151 us
  blocking collectives  58.2 us (38%)
  waiting for transfers between devices  33.5 us (22%)
  other arithmetic  23.7 us (16%)
  local copies, waits for them, and re-layouts  17.9 us (12%)
  starting transfers between devices  14 us (9%)
  between operations  4.22 us (3%)
    all_to_all x2, blocking collectives, exchange_in_order(): lax.all_to_all(tiles, axes[k], split_axis=k, concat_axis=k, tiled=True)  53.3 us
    all_to_all x1, waiting for transfers between devices, body(): lax.all_to_all(ordered, REP, split_axis=0, concat_axis=0, tiled=True)  28.9 us
    add x6, other arithmetic, body(): current = current + step_size * moment  9.21 us
    all_to_all x1, starting transfers between devices, body(): lax.all_to_all(ordered, REP, split_axis=0, concat_axis=0, tiled=True)  8.68 us
    unnamed x19, local copies, waits for them, and re-layouts  5.61 us
    all_to_all x1, blocking collectives, from_everyone(): lax.all_to_all(jnp.broadcast_to(shard[None], (peers, *shard.shape)), axis...  4.94 us
    unnamed x1, other arithmetic  4.57 us
    slice x16, local copies, waits for them, and re-layouts, force_rows(): jnp.roll(centre, 1, 1) + jnp.roll(centre, -1, 1)  3.78 us
  transfers between devices with their start and end apart: 7, of which 5 were waited for; matrix products, arithmetic and copies ran while one was open for 2% of the time, Pallas kernels for 0%

commit v1 on v0

v1 whole, which is shorter than its diff:
```python
import functools
import jax
import jax.numpy as jnp
from jax import lax
from jax.experimental import pallas as pl
from jax.experimental.pallas import tpu as pltpu
from jax.sharding import PartitionSpec as P

STEPS = 8
MESH = pl.DeviceIdType.MESH

hopping = 0.18
quartic = 0.3
step_size = 0.05

def with_halo(cells, sides, width):
    for axis, dim in sides:
        count = lax.axis_size(axis)
        head = lax.slice_in_dim(cells, 0, width, axis=dim)
        tail = lax.slice_in_dim(cells, cells.shape[dim] - width, cells.shape[dim], axis=dim)
        cells = jnp.concatenate(
            [
                lax.ppermute(tail, axis, [(i, (i + 1) % count) for i in range(count)]),
                cells,
                lax.ppermute(head, axis, [((i + 1) % count, i) for i in range(count)]),
            ],
            axis=dim,
        )
    return cells


def force_rows(padded, coldness):
    centre = padded[1:-1]
    beside_all = padded[:-2] + padded[2:] + (jnp.roll(centre, 1, 1) + jnp.roll(centre, -1, 1))
    return coldness * (
        -2.0 * hopping * beside_all
        + 2.0 * centre
        + 4.0 * quartic * centre * (centre * centre - 1.0)
    )


def site_terms(padded, margin, strip_rows):
    values = padded[margin : margin + strip_rows]
    lower_row = padded[margin + 1 : margin + 1 + strip_rows]
    neighbours = lower_row + jnp.roll(values, -1, 1)
    squared = values * values
    return (
        -2.0 * hopping * values * neighbours + squared + quartic * (squared - 1.0) * (squared - 1.0)
    )


def trim_rows(values, margin, target):
    excess = margin - target
    return values[excess : values.shape[0] - excess]


def split_rep(rep):
    return rep // 32, (rep // 4) % 8, (rep // 2) % 2, rep % 2


def join_rep(x, z, y, c):
    return ((x * 8 + z) * 2 + y) * 2 + c


def table_place(rep):
    x, z, y, c = split_rep(rep)
    return ((x * 2 + y) * 2 + c) * 8 + z


def tile_of(ref, chunk, home):
    block = lax.rem(4 + 8 * chunk + lax.div(home, 16), 16)
    rows = pl.ds(pl.multiple_of(block * 8, 8), 8)
    cols = pl.ds(pl.multiple_of(lax.rem(home, 16) * 128, 128), 128)
    return ref.at[0, rows, cols]


def wait_for(ref, sem):
    pltpu.make_async_copy(ref, ref, sem).wait()


def exchange(
    field_ref, info_ref, label_ref,
    sorted_ref, change_ref, ladder_ref,
    got_0, got_1, picked, label_row, label_tab, act_row, act_got, act_sum, act_tab, holder_row, holder_ref,
    send_1, recv_1, send_2, recv_2, send_lab, recv_lab, send_act, recv_act, local_sem,
):
    me = lax.axis_index("rep")
    dom = lax.axis_index("dom")
    other = 1 - dom
    x, z, y, c = split_rep(me)
    place = table_place(me)
    group = lax.div(place, 8)
    got = (got_0, got_1)

    def push(src, dst, send_sem, recv_sem, rep):
        pltpu.make_async_remote_copy(
            src_ref=src, dst_ref=dst, send_sem=send_sem, recv_sem=recv_sem,
            device_id=(rep, other), device_id_type=MESH,
        ).start()

    barrier = pltpu.get_barrier_semaphore()

    def greet(k, carry):
        pl.semaphore_signal(barrier, inc=1, device_id=(lax.rem(me + k, 128), other), device_id_type=MESH)
        return carry

    lax.fori_loop(0, 128, greet, 0)

    def to_column(row, tab, send_sem, recv_sem):
        for k in range(8):
            push(row, tab.at[place], send_sem, recv_sem, join_rep(x, (z + k) % 8, y, c))

    def to_plane(tab, out, send_sem, recv_sem):
        block = pl.ds(pl.multiple_of(group * 8, 8), 8)
        for k in range(16):
            push(
                tab.at[block], out.at[block], send_sem, recv_sem,
                join_rep((x + k // 4) % 4, z, (y + (k // 2) % 2) % 2, (c + k % 2) % 2),
            )

    def spread(chunk):
        def one(k, carry):
            home = lax.rem(me + k, 128)
            push(tile_of(field_ref, chunk, home), got[chunk].at[me], send_1.at[chunk], recv_1.at[chunk], home)
            return carry

        lax.fori_loop(0, 128, one, 0)

    def gather(chunk):
        def pick(t, carry):
            picked[chunk, t] = got[chunk][holder_ref[0, t]]
            return carry

        lax.fori_loop(0, 128, pick, 0, unroll=8)

        def one(k, carry):
            goal = lax.rem(me + k, 128)
            push(picked.at[chunk, goal], tile_of(sorted_ref, chunk, me), send_2.at[chunk], recv_2, goal)
            return carry

        lax.fori_loop(0, 128, one, 0)

    lane = lax.broadcasted_iota(jnp.int32, (1, 128), 1)
    label_row[...] = jnp.full((1, 128), label_ref[0], jnp.int32)
    act_row[...] = info_ref[...]
    pl.semaphore_wait(barrier, 128)

    to_column(label_row, label_tab.at[0], send_lab.at[0], recv_lab.at[0])
    push(act_row, act_got, send_act.at[0], recv_act.at[0], me)
    spread(0)
    wait_for(label_tab.at[0, pl.ds(0, 8)], recv_lab.at[0])
    to_plane(label_tab.at[0], label_tab.at[1], send_lab.at[1], recv_lab.at[1])
    wait_for(act_got, recv_act.at[0])
    total = act_row[...] + act_got[...]
    act_sum[...] = total
    to_column(act_sum, act_tab.at[0], send_act.at[1], recv_act.at[1])
    spread(1)

    wait_for(label_tab.at[1], recv_lab.at[1])
    holder = jnp.zeros((1, 128), jnp.int32)
    for p in range(128):
        rep = join_rep(p // 32, p % 8, (p // 16) % 2, (p // 8) % 2)
        holder = jnp.maximum(holder, jnp.where(label_tab[1, p] == lane, rep, 0))
    holder_row[...] = holder
    copy = pltpu.make_async_copy(holder_row, holder_ref, local_sem)
    copy.start()
    copy.wait()

    wait_for(act_tab.at[0, pl.ds(0, 8)], recv_act.at[1])
    to_plane(act_tab.at[0], act_tab.at[1], send_act.at[2], recv_act.at[2])
    wait_for(got_0, recv_1.at[0])
    gather(0)
    wait_for(got_1, recv_1.at[1])
    gather(1)

    wait_for(act_tab.at[1], recv_act.at[2])
    ladder = jnp.zeros((1, 128), jnp.float32)
    for p in range(128):
        ladder = ladder + jnp.where(label_tab[1, p] == me, act_tab[1, p], 0.0)
    ladder_ref[0] = jnp.sum(jnp.where(lane == 0, ladder, 0.0)) / 524288.0
    change_ref[0] = jnp.sum(jnp.where(lane == 1, total, 0.0))

    wait_for(label_tab.at[0, pl.ds(0, 8)], send_lab.at[0])
    wait_for(label_tab.at[1], send_lab.at[1])
    wait_for(act_got, send_act.at[0])
    wait_for(act_tab.at[0, pl.ds(0, 8)], send_act.at[1])
    wait_for(act_tab.at[1], send_act.at[2])
    for chunk in range(2):
        wait_for(got[chunk], send_1.at[chunk])
        wait_for(got[chunk], send_2.at[chunk])
    wait_for(sorted_ref, recv_2)


def body(field, momentum, labels, betas, accept, swap_pairs):
    strip_rows = field.shape[1]
    ladder_index = jnp.arange(betas.shape[0], dtype=jnp.int32)
    chosen = ladder_index == labels[0]
    coldness = jnp.sum(jnp.where(chosen, betas, 0.0))
    new_label = jnp.sum(jnp.where(chosen, swap_pairs, 0))
    start_field = field[0]
    start_moment = momentum[0]
    current = start_field
    moment = start_moment
    margin = 0
    old_action = None
    new_action = None
    for leap_step in range(STEPS + 1):
        if margin == 0:
            stacked = with_halo(jnp.stack((current, moment)), (("dom", 1),), 3)
            current = stacked[0]
            moment = stacked[1]
            margin = 3
        padded = current
        outer = margin
        if leap_step == 0:
            old_action = site_terms(padded, outer, strip_rows)
        if leap_step == STEPS:
            new_action = site_terms(padded, outer, strip_rows)
        force_now = force_rows(padded, coldness)
        moment = trim_rows(moment, margin, outer - 1)
        current = trim_rows(padded, outer, outer - 1)
        margin = outer - 1
        factor = 0.5 * step_size if leap_step == 0 or leap_step == STEPS else step_size
        moment = moment - factor * force_now
        if leap_step < STEPS:
            current = current + step_size * moment
    change_part = jnp.sum(
        0.5 * moment * moment
        + coldness * new_action
        - (0.5 * start_moment * start_moment + coldness * old_action)
    )
    accepted = accept[0] == 1
    action_part = jnp.where(accepted, jnp.sum(new_action), jnp.sum(old_action))
    field_out = jnp.where(accepted, current, start_field)
    lane = jnp.arange(128)[None]
    info = jnp.where(lane == 0, action_part, jnp.where(lane == 1, change_part, 0.0))
    vmem = pl.BlockSpec(memory_space=pltpu.VMEM)
    smem = pl.BlockSpec(memory_space=pltpu.SMEM)
    f32, i32 = jnp.float32, jnp.int32
    dma = pltpu.SemaphoreType.DMA
    ordered, change, ladder = pl.pallas_call(
        exchange,
        out_shape=(
            jax.ShapeDtypeStruct((1, 128, 2048), f32),
            jax.ShapeDtypeStruct((1,), f32),
            jax.ShapeDtypeStruct((1,), f32),
        ),
        in_specs=[vmem, vmem, smem],
        out_specs=(vmem, smem, smem),
        scratch_shapes=[
            pltpu.VMEM((128, 8, 128), f32),
            pltpu.VMEM((128, 8, 128), f32),
            pltpu.VMEM((2, 128, 8, 128), f32),
            pltpu.VMEM((1, 128), i32),
            pltpu.VMEM((2, 128, 1, 128), i32),
            pltpu.VMEM((1, 128), f32),
            pltpu.VMEM((1, 128), f32),
            pltpu.VMEM((1, 128), f32),
            pltpu.VMEM((2, 128, 1, 128), f32),
            pltpu.VMEM((1, 128), i32),
            pltpu.SMEM((1, 128), i32),
            dma((2,)), dma((2,)), dma((2,)), dma(()), dma((2,)), dma((2,)), dma((3,)), dma((3,)), dma(()),
        ],
        compiler_params=pltpu.CompilerParams(collective_id=0, has_side_effects=True, vmem_limit_bytes=32 << 20),
    )(field_out[None], info, new_label[None])
    return (field_out[None], ordered, new_label[None], change, ladder)


def solution(mesh):
    rep = P("rep")
    strip = P("rep", "dom", None)
    in_specs = (strip, strip, rep, P(), rep, P())
    out_specs = (strip, strip, rep, rep, rep)
    return jax.shard_map(body, mesh=mesh, in_specs=in_specs, out_specs=out_specs, check_vma=False)
```

time: 152 us -> 110 us (0.72)
  Pallas kernels: 0 us -> 65.7 us
  blocking collectives: 58.2 us -> 0 us
  waiting for transfers between devices: 33.5 us -> 5.24 us
  local copies, waits for them, and re-layouts: 17.9 us -> 7.5 us
  starting transfers between devices: 14 us -> 5.41 us
  other arithmetic: 23.7 us -> 18.8 us
  between operations: 4.22 us -> 7.2 us
    pallas_call x0 -> x1, Pallas kernels: none -> 65.7 us  [body(): pl.pallas_call(exchange, out_shape=(jax.ShapeDtypeStruct((1, 128, 2048),...]
    all_to_all x3 -> x0, blocking collectives: 58.2 us -> none  [the longest x2 53.3 us: exchange_in_order(): lax.all_to_all(tiles, axes[k], split_axis=k, concat_axis=k, tiled=True)]
    all_to_all x1 -> x0, waiting for transfers between devices: 28.9 us -> none  [body(): lax.all_to_all(ordered, REP, split_axis=0, concat_axis=0, tiled=True)]
    all_to_all x1 -> x0, starting transfers between devices: 8.68 us -> none  [body(): lax.all_to_all(ordered, REP, split_axis=0, concat_axis=0, tiled=True)]
    unnamed x1 -> x0, other arithmetic: 4.57 us -> none
    reduce_sum x3 -> x1, other arithmetic: 0.24 us -> 3.7 us  [body(): action_part = jnp.where(accepted, jnp.sum(new_action), jnp.sum(old_action))]
    unnamed x19 -> x12, local copies, waits for them, and re-layouts: 5.61 us -> 2.52 us
    gather x1 -> x0, local copies, waits for them, and re-layouts: 1.87 us -> none  [body(): ordered = jnp.take(received, holder, axis=0)]
  transfers between devices with their start and end apart: 7 -> 6, of which waited for: 5 -> 5; matrix products, arithmetic and copies ran while one was open for 2% -> 1% of each run, Pallas kernels for 0% -> 0%
where the time goes in v1:
time: 110 us
  Pallas kernels  65.7 us (60%)
  other arithmetic  18.8 us (17%)
  local copies, waits for them, and re-layouts  7.5 us (7%)
  between operations  7.2 us (7%)
  starting transfers between devices  5.41 us (5%)
  waiting for transfers between devices  5.24 us (5%)
    pallas_call x1, Pallas kernels, body(): pl.pallas_call(exchange, out_shape=(jax.ShapeDtypeStruct((1, 128, 2048),...  65.7 us
    add x6, other arithmetic, body(): current = current + step_size * moment  9.21 us
    slice x18, local copies, waits for them, and re-layouts, force_rows(): jnp.roll(centre, 1, 1) + jnp.roll(centre, -1, 1)  4.24 us
    reduce_sum x1, other arithmetic, body(): action_part = jnp.where(accepted, jnp.sum(new_action), jnp.sum(old_action))  3.7 us
    ppermute x3, starting transfers between devices, with_halo(): lax.ppermute(head, axis, [((i + 1) % count, i) for i in range(count)])  3.3 us
    ppermute x3, waiting for transfers between devices, with_halo(): lax.ppermute(tail, axis, [(i, (i + 1) % count) for i in range(count)])  3.12 us
    another operation x2, other arithmetic, body(): stacked = with_halo(jnp.stack((current, moment)), (('dom', 1),), 3)  2.94 us
    unnamed x12, local copies, waits for them, and re-layouts  2.52 us
  transfers between devices with their start and end apart: 6, of which 5 were waited for; matrix products, arithmetic and copies ran while one was open for 1% of the time, Pallas kernels for 0%

profile of v1, /device:TPU:1, one launch (start us, length us, event | category | flops | bytes accessed | tf_op | source)
XLA Modules:
  0.0 109.9 jit_solution(5772652747479307166)
XLA Ops:
  0.6 1.4 %constant_dynamic-update-slice_fusion.1 = f32[2,128,2048]{2,1,0:T(8,128)S(1)} fusion(f32[1,128,2048]{2,1,0:T(8,128)} %param.6), kind=kLoop, calls=%fused_computation.125 | loop fusion | bytes 2097152
  2.3 2.2 %collective-permute-start.1 = (f32[2,3,2048]{2,1,0:T(4,128)S(1)}, f32[2,3,2048]{2,1,0:T(4,128)S(1)}, u32[]{:S(2)}, u32[]{:S(2)}) collective-permute-start(f32[2,3,2048]{2,1,0:T(4,128)S(1)} %get-tuple-element.35), channel_id=1, source_target_pairs={{1,0},{0,1},{3,2},{2,3},{5,4},{4,5},{7,6},{6,7},{9,8},{8,9},{11,10... | collective-permute-start | bytes 147464 | tf_op jit(solution)/shard_map/ppermute | solution.py:25
  5.3 0.6 fusion.77
  6.2 1.5 %collective-permute-done = f32[2,3,2048]{2,1,0:T(4,128)S(1)} collective-permute-done((f32[2,3,2048]{2,1,0:T(4,128)S(1)}, f32[2,3,2048]{2,1,0:T(4,128)S(1)}, u32[]{:S(2)}, u32[]{:S(2)}) %collective-permute-start) | collective-permute-done | bytes 49184 | tf_op jit(solution)/shard_map/ppermute | solution.py:23
  8.1 0.4 fusion.105
  8.5 1.5 %multiply_add_fusion.5 = (f32[132,2048]{1,0:T(8,128)S(1)}, f32[132,2048]{1,0:T(8,128)S(1)}) fusion(f32[2,134,2048]{2,1,0:T(8,128)S(1)} %pad_maximum_fusion, f32[132,1]{1,0:T(8,128)S(1)} %get-tuple-element.70, f32[132,2047]{1,0:T(8,128)S(1)} %get-tuple-element.72, f32[132,2047]{1,0:T(8,128)S(1)} %get-tuple-element.71, f32[132,1]{1,0:T(8,128)S(1)} %get-tuple-element.69, ...), kind=kLoop, calls=%fused_computation.75 | loop fusion | flops 4866048 | bytes 8650756 | tf_op jit(solution)/shard_map/add | solution.py:226
  10.1 0.4 fusion.103
  10.6 1.5 %multiply_add_fusion.4 = (f32[130,2048]{1,0:T(8,128)S(1)}, f32[130,2048]{1,0:T(8,128)S(1)}) fusion(f32[132,2048]{1,0:T(8,128)S(1)} %get-tuple-element.28, f32[130,1]{1,0:T(8,128)S(1)} %get-tuple-element.66, f32[130,2047]{1,0:T(8,128)S(1)} %get-tuple-element.68, f32[130,2047]{1,0:T(8,128)S(1)} %get-tuple-element.67, f32[130,1]{1,0:T(8,128)S(1)} %get-tuple-element.65, ...), kind=kLoop, calls=%fused_computation.74 | loop fusion | flops 4792320 | bytes 8519684 | tf_op jit(solution)/shard_map/add | solution.py:226
  12.1 0.4 fusion.101
  12.6 1.5 %add_bitcast_fusion.1 = (f32[1,128,2048]{2,1,0:T(8,128)S(1)}, f32[128,2048]{1,0:T(8,128)S(1)}) fusion(f32[130,2048]{1,0:T(8,128)S(1)} %get-tuple-element.26, f32[128,1]{1,0:T(8,128)S(1)} %get-tuple-element.62, f32[128,2047]{1,0:T(8,128)S(1)} %get-tuple-element.64, f32[128,2047]{1,0:T(8,128)S(1)} %get-tuple-element.63, f32[128,1]{1,0:T(8,128)S(1)} %get-tuple-element.61, ...), kind=kLoop, calls=%fused_computation.119 | loop fusion | flops 4718592 | bytes 8388612 | tf_op jit(solution)/shard_map/stack | solution.py:209
  14.1 1.2 %collective-permute-start.2 = (f32[2,3,2048]{2,1,0:T(4,128)S(1)}, f32[2,3,2048]{2,1,0:T(4,128)S(1)}, u32[]{:S(2)}, u32[]{:S(2)}) collective-permute-start(f32[2,3,2048]{2,1,0:T(4,128)S(1)} %get-tuple-element.32), channel_id=1, source_target_pairs={{0,1},{1,0},{2,3},{3,2},{4,5},{5,4},{6,7},{7,6},{8,9},{9,8},{10,11... | collective-permute-start | bytes 147464 | tf_op jit(solution)/shard_map/ppermute | solution.py:23
  15.7 1.6 %collective-permute-done.2 = f32[2,3,2048]{2,1,0:T(4,128)S(1)} collective-permute-done((f32[2,3,2048]{2,1,0:T(4,128)S(1)}, f32[2,3,2048]{2,1,0:T(4,128)S(1)}, u32[]{:S(2)}, u32[]{:S(2)}) %collective-permute-start.2) | collective-permute-done | bytes 49184 | tf_op jit(solution)/shard_map/ppermute | solution.py:23
  17.3 1.1 %collective-permute-done.3 = f32[2,3,2048]{2,1,0:T(4,128)S(1)} collective-permute-done((f32[2,3,2048]{2,1,0:T(4,128)S(1)}, f32[2,3,2048]{2,1,0:T(4,128)S(1)}, u32[]{:S(2)}, u32[]{:S(2)}) %collective-permute-start.3) | collective-permute-done | bytes 49184 | tf_op jit(solution)/shard_map/ppermute | solution.py:25
  18.9 0.4 fusion.99
  19.3 1.5 %multiply_add_fusion.3 = (f32[132,2048]{1,0:T(8,128)S(1)}, f32[132,2048]{1,0:T(8,128)S(1)}) fusion(f32[2,134,2048]{2,1,0:T(8,128)S(1)} %pad_maximum_fusion.1, f32[132,1]{1,0:T(8,128)S(1)} %get-tuple-element.58, f32[132,2047]{1,0:T(8,128)S(1)} %get-tuple-element.60, f32[132,2047]{1,0:T(8,128)S(1)} %get-tuple-element.59, f32[132,1]{1,0:T(8,128)S(1)} %get-tuple-element.57, ...), kind=kLoop, calls=%fused_computation.73 | loop fusion | flops 4866048 | bytes 8650756 | tf_op jit(solution)/shard_map/add | solution.py:226
  20.9 0.4 fusion.97
  21.4 1.5 %multiply_add_fusion.2 = (f32[130,2048]{1,0:T(8,128)S(1)}, f32[130,2048]{1,0:T(8,128)S(1)}) fusion(f32[132,2048]{1,0:T(8,128)S(1)} %get-tuple-element.22, f32[130,1]{1,0:T(8,128)S(1)} %get-tuple-element.54, f32[130,2047]{1,0:T(8,128)S(1)} %get-tuple-element.56, f32[130,2047]{1,0:T(8,128)S(1)} %get-tuple-element.55, f32[130,1]{1,0:T(8,128)S(1)} %get-tuple-element.53, ...), kind=kLoop, calls=%fused_computation.72 | loop fusion | flops 4792320 | bytes 8519684 | tf_op jit(solution)/shard_map/add | solution.py:226
  22.9 0.4 fusion.95
  23.4 1.5 %add_bitcast_fusion = (f32[1,128,2048]{2,1,0:T(8,128)S(1)}, f32[128,2048]{1,0:T(8,128)S(1)}) fusion(f32[130,2048]{1,0:T(8,128)S(1)} %get-tuple-element.20, f32[128,1]{1,0:T(8,128)S(1)} %get-tuple-element.50, f32[128,2047]{1,0:T(8,128)S(1)} %get-tuple-element.52, f32[128,2047]{1,0:T(8,128)S(1)} %get-tuple-element.51, f32[128,1]{1,0:T(8,128)S(1)} %get-tuple-element.49, ...), kind=kLoop, calls=%fused_computation.118 | loop fusion | flops 4718592 | bytes 8388612 | tf_op jit(solution)/shard_map/stack | solution.py:209
  24.9 0.8 collective-permute-start.4
  25.7 0.8 collective-permute-start.5
  26.5 0.6 fusion.78
  28.2 0.7 collective-permute-done.5
  29.3 0.4 fusion.93
  29.8 1.5 %multiply_add_fusion.1 = (f32[132,2048]{1,0:T(8,128)S(1)}, f32[132,2048]{1,0:T(8,128)S(1)}) fusion(f32[2,134,2048]{2,1,0:T(8,128)S(1)} %pad_maximum_fusion.2, f32[132,1]{1,0:T(8,128)S(1)} %get-tuple-element.46, f32[132,2047]{1,0:T(8,128)S(1)} %get-tuple-element.48, f32[132,2047]{1,0:T(8,128)S(1)} %get-tuple-element.47, f32[132,1]{1,0:T(8,128)S(1)} %get-tuple-element.45, ...), kind=kLoop, calls=%fused_computation.71 | loop fusion | flops 4866048 | bytes 8650756 | tf_op jit(solution)/shard_map/add | solution.py:226
  31.3 0.4 fusion.91
  31.8 1.5 %multiply_add_fusion = (f32[130,2048]{1,0:T(8,128)S(1)}, f32[130,2048]{1,0:T(8,128)S(1)}) fusion(f32[132,2048]{1,0:T(8,128)S(1)} %get-tuple-element.16, f32[130,1]{1,0:T(8,128)S(1)} %get-tuple-element.42, f32[130,2047]{1,0:T(8,128)S(1)} %get-tuple-element.44, f32[130,2047]{1,0:T(8,128)S(1)} %get-tuple-element.43, f32[130,1]{1,0:T(8,128)S(1)} %get-tuple-element.41, ...), kind=kLoop, calls=%fused_computation.70 | loop fusion | flops 4792320 | bytes 8519684 | tf_op jit(solution)/shard_map/add | solution.py:226
  33.3 0.4 fusion.89
  33.8 3.7 %fusion.76 = (f32[]{:T(128)}, f32[]{:T(128)}, f32[]{:T(128)}, f32[1,128,2048]{2,1,0:T(8,128)S(1)}) fusion(f32[130,2048]{1,0:T(8,128)S(1)} %get-tuple-element.14, f32[128,1]{1,0:T(8,128)S(1)} %get-tuple-element.38, f32[128,2047]{1,0:T(8,128)S(1)} %get-tuple-element.40, f32[1,128,2048]{2,1,0:T(8,128)S(1)} %copy-done.2, f32[128,2047]{1,0:T(8,128)S(1)} %get-tuple-element.39, ...), kind=kLoop, calls=%fused_computation.115 | loop fusion | flops 12320765 | bytes 12632081 | tf_op jit(solution)/shard_map/reduce_sum | solution.py:233
  38.9 0.7 compare_select_fusion.1.info_ref
  39.6 65.7 %shard_map.101 = (f32[1,128,2048]{2,1,0:T(8,128)S(1)}, f32[1]{0:T(128)}, f32[1]{0:T(128)}) custom-call(f32[1,128,2048]{2,1,0:T(8,128)S(1)} %get-tuple-element.78.field_ref, f32[1,128]{1,0:T(1,128)S(1)} %compare_select_fusion.1.info_ref, s32[1]{0:T(128)} %bitcast.19.label_ref), custom_call_target="tpu_custom_call" | custom-call | tf_op jit(solution)/shard_map/pallas_call | solution.py:241
  105.3 1.0 copy.17
  (35 shorter events, 3.4 us)
Async XLA Ops:
  0.6 1.5 %copy-start.2 = (f32[1,128,2048]{2,1,0:T(8,128)S(1)}, f32[1,128,2048]{2,1,0:T(8,128)}, u32[]{:S(2)}) copy-start(f32[1,128,2048]{2,1,0:T(8,128)} %param.7) | copy-start | bytes 3145732
  2.2 3.1 %copy-start.3 = (f32[128]{0:T(128)S(1)}, f32[128]{0:T(128)}, u32[]{:S(2)}) copy-start(f32[128]{0:T(128)} %param.9) | copy-start | bytes 1540
  2.3 3.9 %collective-permute-start.1 = (f32[2,3,2048]{2,1,0:T(4,128)S(1)}, f32[2,3,2048]{2,1,0:T(4,128)S(1)}, u32[]{:S(2)}, u32[]{:S(2)}) collective-permute-start(f32[2,3,2048]{2,1,0:T(4,128)S(1)} %get-tuple-element.35), channel_id=1, source_target_pairs={{1,0},{0,1},{3,2},{2,3},{5,4},{4,5},{7,6},{6,7},{9,8},{8,9},{11,10... | collective-permute-start | bytes 147464 | tf_op jit(solution)/shard_map/ppermute | solution.py:25
  4.5 3.1 %collective-permute-start = (f32[2,3,2048]{2,1,0:T(4,128)S(1)}, f32[2,3,2048]{2,1,0:T(4,128)S(1)}, u32[]{:S(2)}, u32[]{:S(2)}) collective-permute-start(f32[2,3,2048]{2,1,0:T(4,128)S(1)} %get-tuple-element.34), channel_id=1, source_target_pairs={{0,1},{1,0},{2,3},{3,2},{4,5},{5,4},{6,7},{7,6},{8,9},{9,8},{10,11... | collective-permute-start | bytes 147464 | tf_op jit(solution)/shard_map/ppermute | solution.py:23
  14.1 3.2 %collective-permute-start.2 = (f32[2,3,2048]{2,1,0:T(4,128)S(1)}, f32[2,3,2048]{2,1,0:T(4,128)S(1)}, u32[]{:S(2)}, u32[]{:S(2)}) collective-permute-start(f32[2,3,2048]{2,1,0:T(4,128)S(1)} %get-tuple-element.32), channel_id=1, source_target_pairs={{0,1},{1,0},{2,3},{3,2},{4,5},{5,4},{6,7},{7,6},{8,9},{9,8},{10,11... | collective-permute-start | bytes 147464 | tf_op jit(solution)/shard_map/ppermute | solution.py:23
  15.3 3.1 %collective-permute-start.3 = (f32[2,3,2048]{2,1,0:T(4,128)S(1)}, f32[2,3,2048]{2,1,0:T(4,128)S(1)}, u32[]{:S(2)}, u32[]{:S(2)}) collective-permute-start(f32[2,3,2048]{2,1,0:T(4,128)S(1)} %get-tuple-element.33), channel_id=1, source_target_pairs={{1,0},{0,1},{3,2},{2,3},{5,4},{4,5},{7,6},{6,7},{9,8},{8,9},{11,10... | collective-permute-start | bytes 147464 | tf_op jit(solution)/shard_map/ppermute | solution.py:25
  24.9 1.6 %copy-start.4 = (s32[128]{0:T(128)S(1)}, s32[128]{0:T(128)}, u32[]{:S(2)}) copy-start(s32[128]{0:T(128)} %param.11) | copy-start | bytes 1540
  24.9 2.2 %copy-start.1 = (f32[1,128,2048]{2,1,0:T(8,128)S(1)}, f32[1,128,2048]{2,1,0:T(8,128)}, u32[]{:S(2)}) copy-start(f32[1,128,2048]{2,1,0:T(8,128)} %param.6) | copy-start | bytes 3145732
  24.9 3.2 %collective-permute-start.4 = (f32[2,3,2048]{2,1,0:T(4,128)S(1)}, f32[2,3,2048]{2,1,0:T(4,128)S(1)}, u32[]{:S(2)}, u32[]{:S(2)}) collective-permute-start(f32[2,3,2048]{2,1,0:T(4,128)S(1)} %get-tuple-element.30), channel_id=1, source_target_pairs={{0,1},{1,0},{2,3},{3,2},{4,5},{5,4},{6,7},{7,6},{8,9},{9,8},{10,11... | collective-permute-start | bytes 147464 | tf_op jit(solution)/shard_map/ppermute | solution.py:23
  25.7 3.1 %collective-permute-start.5 = (f32[2,3,2048]{2,1,0:T(4,128)S(1)}, f32[2,3,2048]{2,1,0:T(4,128)S(1)}, u32[]{:S(2)}, u32[]{:S(2)}) collective-permute-start(f32[2,3,2048]{2,1,0:T(4,128)S(1)} %get-tuple-element.31), channel_id=1, source_target_pairs={{1,0},{0,1},{3,2},{2,3},{5,4},{4,5},{7,6},{6,7},{9,8},{8,9},{11,10... | collective-permute-start | bytes 147464 | tf_op jit(solution)/shard_map/ppermute | solution.py:25
  37.5 68.7 %copy-start = (f32[1,128,2048]{2,1,0:T(8,128)}, f32[1,128,2048]{2,1,0:T(8,128)S(1)}, u32[]{:S(2)}) copy-start(f32[1,128,2048]{2,1,0:T(8,128)S(1)} %get-tuple-element.78.field_ref) | copy-start | bytes 3145732

commit v2 on v1

v2 whole, which is shorter than its diff:
```python
import functools
import jax
import jax.numpy as jnp
from jax import lax
from jax.experimental import pallas as pl
from jax.experimental.pallas import tpu as pltpu
from jax.sharding import PartitionSpec as P

MESH = pl.DeviceIdType.MESH

HOP = 0.36
QUARTIC = 0.3
EPS = 0.05
F32 = jnp.float32
BF16 = jnp.bfloat16

def split_rep(rep):
    return rep // 32, (rep // 4) % 8, (rep // 2) % 2, rep % 2


def join_rep(x, z, y, c):
    return ((x * 8 + z) * 2 + y) * 2 + c


def table_place(rep):
    x, z, y, c = split_rep(rep)
    return ((x * 2 + y) * 2 + c) * 8 + z


def tile_of(ref, chunk, home):
    block = lax.rem(4 + 8 * chunk + lax.div(home, 16), 16)
    rows = pl.ds(pl.multiple_of(block * 8, 8), 8)
    cols = pl.ds(pl.multiple_of(lax.rem(home, 16) * 128, 128), 128)
    return ref.at[0, rows, cols]


def wait_for(ref, sem):
    pltpu.make_async_copy(ref, ref, sem).wait()


def rows_of(block):
    return pl.ds(pl.multiple_of(block * 8, 8), 8)


def lateral(q):
    even, odd = q[:, :1024], q[:, 1024:]
    after = pltpu.roll(even, 1023, 1)
    return jnp.concatenate((odd + pltpu.roll(odd, 1, 1), even + after), 1), jnp.concatenate((odd, after), 1)


def fold(v):
    total = v[:, :128]
    for j in range(1, 16):
        total = total + v[:, 128 * j : 128 * j + 128]
    return total


def split_two(v):
    high = v.astype(BF16)
    return high, (v - high.astype(F32)).astype(BF16)


def site(q, below, right):
    squared = q * q
    return -HOP * q * (below + right) + squared + QUARTIC * (squared - 1.0) * (squared - 1.0)


def whole(
    field_ref, moment_ref, labels_ref, betas_ref, accept_ref, pairs_ref,
    out_ref, sorted_ref, new_ref, change_ref, ladder_ref,
    q0, m0, qa, pa, qe, pe, perm, perm_back,
    got_0, got_1, picked, label_row, label_tab, act_row, act_got, act_sum, act_tab, holder_row, holder_ref,
    send_h, recv_h, send_1, recv_1, send_2, recv_2, send_lab, recv_lab, send_act, recv_act, local_sem,
):
    me = lax.axis_index("rep")
    dom = lax.axis_index("dom")
    other = 1 - dom
    x, z, y, c = split_rep(me)
    place = table_place(me)
    group = lax.div(place, 8)
    got = (got_0, got_1)

    def push(src, dst, send_sem, recv_sem, rep):
        pltpu.make_async_remote_copy(
            src_ref=src, dst_ref=dst, send_sem=send_sem, recv_sem=recv_sem,
            device_id=(rep, other), device_id_type=MESH,
        ).start()

    barrier = pltpu.get_barrier_semaphore()

    def greet(k, carry):
        pl.semaphore_signal(barrier, inc=1, device_id=(lax.rem(me + k, 128), other), device_id_type=MESH)
        return carry

    lax.fori_loop(0, 128, greet, 0, unroll=8)

    label = labels_ref[0]
    coldness = betas_ref[label]
    new_label = pairs_ref[label]
    accepted = accept_ref[0] == 1
    new_ref[0] = new_label
    label_row[...] = jnp.full((1, 128), new_label, jnp.int32)

    i0 = lax.broadcasted_iota(jnp.int32, (256, 256), 0)
    i1 = lax.broadcasted_iota(jnp.int32, (256, 256), 1)
    there = jnp.where(i1 < 128, 2 * i1, 2 * i1 - 255) == i0
    back = jnp.where(i0 < 128, 2 * i0, 2 * i0 - 255) == i1
    for third in range(3):
        perm[pl.ds(256 * third, 256), :] = jnp.where(there, 1.0, 0.0).astype(BF16)
    for half in range(2):
        perm_back[pl.ds(256 * half, 256), :] = jnp.where(back, 1.0, 0.0).astype(BF16)

    def apart(ref, dst, r):
        values = ref[0, pl.ds(pl.multiple_of(32 * r, 32), 32), :]
        high = values.astype(BF16)
        pieces = (high, *split_two(values - high.astype(F32)))
        cols = [slice(256 * b, 256 * b + 256) for b in range(8)]
        left = jnp.concatenate([jnp.concatenate([v[:, s] for v in pieces], 1) for s in cols], 0)
        res = jnp.dot(left, perm[...], preferred_element_type=F32)
        rows = pl.ds(pl.multiple_of(16 + 32 * r, 16), 32)
        for b in range(8):
            dst[rows, 128 * b : 128 * b + 128] = res[32 * b : 32 * b + 32, :128]
            dst[rows, 1024 + 128 * b : 1152 + 128 * b] = res[32 * b : 32 * b + 32, 128:]

    def joined(values):
        high, low = split_two(values)
        parts = []
        for b in range(8):
            e = slice(128 * b, 128 * b + 128)
            o = slice(1024 + 128 * b, 1152 + 128 * b)
            parts.append(jnp.concatenate((high[:, e], high[:, o], low[:, e], low[:, o]), 1))
        res = jnp.dot(jnp.concatenate(parts, 0), perm_back[...], preferred_element_type=F32)
        return jnp.concatenate([res[32 * b : 32 * b + 32] for b in range(8)], 1)

    def settle(values, rows):
        for at, n, first in rows:
            old = field_ref[0, pl.ds(first, n), :]
            out_ref[0, pl.ds(first, n), :] = jnp.where(accepted, values[at : at + n], old)

    def set_apart(r, carry):
        apart(field_ref, q0, r)
        apart(moment_ref, m0, r)
        return carry

    lax.fori_loop(0, 4, set_apart, 0)

    row = lax.broadcasted_iota(jnp.int32, (8, 2048), 0)
    a = coldness * (EPS * EPS * HOP)
    b = coldness * (EPS * EPS * (2.0 - 4.0 * QUARTIC))
    g = coldness * (EPS * EPS * 4.0 * QUARTIC)

    def around(ref, block):
        q = ref[rows_of(block), :]
        above = pltpu.roll(jnp.where(row == 7, ref[rows_of(block - 1), :], q), 1, 0)
        below = pltpu.roll(jnp.where(row == 0, ref[rows_of(block + 1), :], q), 7, 0)
        return q, above, below

    def kicked(q, above, below, beside, moment, share):
        near = (above + below) + beside
        return moment + (near * (share * a) - q * (q * q * (share * g) + share * b))

    def leap(src, src_at, mom, mom_at, dst, dst_p, at, first):
        q, above, below = around(src, src_at)
        beside, _ = lateral(q)
        moment = mom[rows_of(mom_at), :]
        moment = kicked(q, above, below, beside, moment * EPS if first else moment, 0.5 if first else 1.0)
        dst_p[rows_of(at), :] = moment
        dst[rows_of(at), :] = q + moment

    def finish(src, src_at, mom, mom_at, start_at, sums):
        q, above, below = around(src, src_at)
        beside, right = lateral(q)
        moment = kicked(q, above, below, beside, mom[rows_of(mom_at), :], 0.5)
        new = site(q, below, right)
        p, _, p_below = around(q0, start_at)
        old = site(p, p_below, lateral(p)[1])
        start = m0[rows_of(start_at), :]
        change = (moment * moment * (0.5 / (EPS * EPS)) + coldness * new) - (0.5 * start * start + coldness * old)
        return sums[0] + fold(change), sums[1] + fold(jnp.where(accepted, new, old))

    def inner_first(i, carry):
        leap(q0, i, m0, i, qa.at[0], pa, i, True)
        return carry

    lax.fori_loop(3, 17, inner_first, 0)

    def inner(s, carry):
        cur = lax.rem(s - 1, 2)

        def one(i, inside):
            leap(qa.at[cur], i, pa, i, qa.at[1 - cur], pa, i, False)
            return inside

        return lax.fori_loop(3, 17, one, carry)

    lax.fori_loop(1, 8, inner, 0)
    zero = jnp.zeros((8, 128), F32)
    for part in range(2):
        first = 32 + 32 * part
        settle(joined(qa[1, pl.ds(16 + first, 32), :]), [(0, 32, first)])

    def to_column(src, tab, send_sem, recv_sem):
        for k in range(8):
            push(src, tab.at[place], send_sem, recv_sem, join_rep(x, (z + k) % 8, y, c))

    def to_plane(tab, dst, send_sem, recv_sem):
        block = pl.ds(pl.multiple_of(group * 8, 8), 8)
        for k in range(16):
            push(
                tab.at[block], dst.at[block], send_sem, recv_sem,
                join_rep((x + k // 4) % 4, z, (y + (k // 2) % 2) % 2, (c + k % 2) % 2),
            )

    def spread(chunk):
        def one(k, carry):
            home = lax.rem(me + k, 128)
            push(tile_of(out_ref, chunk, home), got[chunk].at[me], send_1.at[chunk], recv_1.at[chunk], home)
            return carry

        lax.fori_loop(0, 128, one, 0, unroll=4)

    def gather(chunk):
        def pick(t, carry):
            picked[chunk, t] = got[chunk][holder_ref[0, t]]
            return carry

        lax.fori_loop(0, 128, pick, 0, unroll=8)

        def one(k, carry):
            goal = lax.rem(me + k, 128)
            push(picked.at[chunk, goal], tile_of(sorted_ref, chunk, me), send_2.at[chunk], recv_2, goal)
            return carry

        lax.fori_loop(0, 128, one, 0, unroll=4)

    halos = ((q0, 136, 8, 8), (q0, 16, 144, 8), (m0, 136, 8, 8), (m0, 16, 144, 8), (q0, 135, 7, 1), (q0, 24, 152, 1))
    pl.semaphore_wait(barrier, 128)
    to_column(label_row, label_tab.at[0], send_lab.at[0], recv_lab.at[0])
    for k, (ref, src_row, dst_row, n) in enumerate(halos):
        push(ref.at[pl.ds(src_row, n)], ref.at[pl.ds(dst_row, n)], send_h.at[k], recv_h.at[k], me)
    spread(0)
    wait_for(label_tab.at[0, pl.ds(0, 8)], recv_lab.at[0])
    to_plane(label_tab.at[0], label_tab.at[1], send_lab.at[1], recv_lab.at[1])

    def inner_last(i, sums):
        return finish(qa.at[1], i, pa, i, i, sums)

    sums = lax.fori_loop(4, 16, inner_last, (zero, zero))
    settle(
        joined(jnp.concatenate((qa[1, pl.ds(32, 16), :], qa[1, pl.ds(112, 16), :]), 0)),
        [(0, 16, 16), (16, 16, 96)],
    )
    for k, (ref, src_row, dst_row, n) in enumerate(halos):
        wait_for(ref.at[pl.ds(dst_row, n)], recv_h.at[k])

    def outer_first(i, carry):
        side, local = lax.div(i, 4), 1 + lax.rem(i, 4)
        leap(q0, 14 * side + local, m0, 14 * side + local, qe.at[0], pe, 6 * side + local, True)
        return carry

    lax.fori_loop(0, 8, outer_first, 0)

    def outer(s, carry):
        cur = lax.rem(s - 1, 2)

        def one(i, inside):
            at = 6 * lax.div(i, 4) + 1 + lax.rem(i, 4)
            leap(qe.at[cur], at, pe, at, qe.at[1 - cur], pe, at, False)
            return inside

        return lax.fori_loop(0, 8, one, carry)

    lax.fori_loop(1, 8, outer, 0)
    settle(
        joined(jnp.concatenate((qe[1, pl.ds(16, 16), :], qe[1, pl.ds(64, 16), :]), 0)),
        [(0, 16, 0), (16, 16, 112)],
    )
    spread(1)

    def outer_last(i, sums):
        side, local = lax.div(i, 2), 2 + lax.rem(i, 2)
        return finish(qe.at[1], 6 * side + local, pe, 6 * side + local, 14 * side + local, sums)

    sums = lax.fori_loop(0, 4, outer_last, sums)
    lane = lax.broadcasted_iota(jnp.int32, (1, 128), 1)
    act_row[...] = jnp.where(lane == 0, jnp.sum(sums[1]), jnp.where(lane == 1, jnp.sum(sums[0]), 0.0))
    push(act_row, act_got, send_act.at[0], recv_act.at[0], me)

    wait_for(label_tab.at[1], recv_lab.at[1])
    holder = jnp.zeros((1, 128), jnp.int32)
    for p in range(128):
        rep = join_rep(p // 32, p % 8, (p // 16) % 2, (p // 8) % 2)
        holder = jnp.maximum(holder, jnp.where(label_tab[1, p] == lane, rep, 0))
    holder_row[...] = holder
    copy = pltpu.make_async_copy(holder_row, holder_ref, local_sem)
    copy.start()
    copy.wait()

    wait_for(got_0, recv_1.at[0])
    gather(0)
    wait_for(act_got, recv_act.at[0])
    total = act_row[...] + act_got[...]
    act_sum[...] = total
    to_column(act_sum, act_tab.at[0], send_act.at[1], recv_act.at[1])
    wait_for(got_1, recv_1.at[1])
    gather(1)
    wait_for(act_tab.at[0, pl.ds(0, 8)], recv_act.at[1])
    to_plane(act_tab.at[0], act_tab.at[1], send_act.at[2], recv_act.at[2])

    for k, (ref, src_row, dst_row, n) in enumerate(halos):
        wait_for(ref.at[pl.ds(src_row, n)], send_h.at[k])
    wait_for(label_tab.at[0, pl.ds(0, 8)], send_lab.at[0])
    wait_for(label_tab.at[1], send_lab.at[1])
    wait_for(act_got, send_act.at[0])
    wait_for(act_tab.at[0, pl.ds(0, 8)], send_act.at[1])
    for chunk in range(2):
        wait_for(got[chunk], send_1.at[chunk])
    change_ref[0] = jnp.sum(jnp.where(lane == 1, total, 0.0))
    wait_for(act_tab.at[1], recv_act.at[2])
    ladder = jnp.zeros((1, 128), F32)
    for p in range(128):
        ladder = ladder + jnp.where(label_tab[1, p] == me, act_tab[1, p], 0.0)
    ladder_ref[0] = jnp.sum(jnp.where(lane == 0, ladder, 0.0)) / 524288.0
    wait_for(act_tab.at[1], send_act.at[2])
    for chunk in range(2):
        wait_for(got[chunk], send_2.at[chunk])
    wait_for(sorted_ref, recv_2)


def body(field, momentum, labels, betas, accept, swap_pairs):
    vmem = pl.BlockSpec(memory_space=pltpu.VMEM)
    smem = pl.BlockSpec(memory_space=pltpu.SMEM)
    i32 = jnp.int32
    dma = pltpu.SemaphoreType.DMA
    strip = jax.ShapeDtypeStruct((1, 128, 2048), F32)
    out, ordered, new_label, change, ladder = pl.pallas_call(
        whole,
        out_shape=(
            strip, strip, jax.ShapeDtypeStruct((1,), i32),
            jax.ShapeDtypeStruct((1,), F32), jax.ShapeDtypeStruct((1,), F32),
        ),
        in_specs=[vmem, vmem, smem, smem, smem, smem],
        out_specs=(vmem, vmem, smem, smem, smem),
        scratch_shapes=[
            pltpu.VMEM((160, 2048), F32),
            pltpu.VMEM((160, 2048), F32),
            pltpu.VMEM((2, 160, 2048), F32),
            pltpu.VMEM((160, 2048), F32),
            pltpu.VMEM((2, 96, 2048), F32),
            pltpu.VMEM((96, 2048), F32),
            pltpu.VMEM((768, 256), BF16),
            pltpu.VMEM((512, 256), BF16),
            pltpu.VMEM((128, 8, 128), F32),
            pltpu.VMEM((128, 8, 128), F32),
            pltpu.VMEM((2, 128, 8, 128), F32),
            pltpu.VMEM((1, 128), i32),
            pltpu.VMEM((2, 128, 1, 128), i32),
            pltpu.VMEM((1, 128), F32),
            pltpu.VMEM((1, 128), F32),
            pltpu.VMEM((1, 128), F32),
            pltpu.VMEM((2, 128, 1, 128), F32),
            pltpu.VMEM((1, 128), i32),
            pltpu.SMEM((1, 128), i32),
            dma((6,)), dma((6,)), dma((2,)), dma((2,)), dma((2,)), dma(()),
            dma((2,)), dma((2,)), dma((3,)), dma((3,)), dma(()),
        ],
        compiler_params=pltpu.CompilerParams(collective_id=0, has_side_effects=True, vmem_limit_bytes=48 << 20),
    )(field, momentum, labels, betas, accept, swap_pairs)
    return out, ordered, new_label, change, ladder


def solution(mesh):
    rep = P("rep")
    strip = P("rep", "dom", None)
    in_specs = (strip, strip, rep, P(), rep, P())
    out_specs = (strip, strip, rep, rep, rep)
    return jax.shard_map(body, mesh=mesh, in_specs=in_specs, out_specs=out_specs, check_vma=False)
```

time: 110 us -> 90.4 us (0.82)
  other arithmetic: 18.8 us -> 0 us
  Pallas kernels: 65.7 us -> 78.6 us
  starting transfers between devices: 5.41 us -> 0 us
  waiting for transfers between devices: 5.24 us -> 0 us
  local copies, waits for them, and re-layouts: 7.5 us -> 4.39 us
    pallas_call x1, Pallas kernels: 65.7 us -> 78.6 us  [body(): pl.pallas_call(whole, out_shape=(strip, strip, jax.ShapeDtypeStruct((1,),...]
    add x6 -> x0, other arithmetic: 9.21 us -> none  [body(): current = current + step_size * moment]
    ppermute x6 -> x0, starting transfers between devices: 5.41 us -> none  [the longest x3 3.3 us: with_halo(): lax.ppermute(head, axis, [((i + 1) % count, i) for i in range(count)])]
    ppermute x6 -> x0, waiting for transfers between devices: 5.24 us -> none  [the longest x3 3.12 us: with_halo(): lax.ppermute(tail, axis, [(i, (i + 1) % count) for i in range(count)])]
    reduce_sum x3 -> x0, other arithmetic: 4.93 us -> none  [the longest x1 3.7 us: body(): action_part = jnp.where(accepted, jnp.sum(new_action), jnp.sum(old_action))]
    slice x24 -> x0, local copies, waits for them, and re-layouts: 4.89 us -> none  [the longest x18 4.24 us: force_rows(): jnp.roll(centre, 1, 1) + jnp.roll(centre, -1, 1)]
    another operation x2 -> x0, other arithmetic: 2.94 us -> none  [body(): stacked = with_halo(jnp.stack((current, moment)), (('dom', 1),), 3)]
    unnamed x12 -> x10, local copies, waits for them, and re-layouts: 2.52 us -> 4.39 us
  transfers between devices with their start and end apart: 6 -> 0, of which waited for: 5 -> 0; matrix products, arithmetic and copies ran while one was open for 1% -> 0% of each run, Pallas kernels for 0% -> 0%
where the time goes in v2:
time: 90.4 us; the launch traced here: 90.2 us
  Pallas kernels  78.6 us (87%)
  between operations  7.24 us (8%)
  local copies, waits for them, and re-layouts  4.39 us (5%)
    pallas_call x1, Pallas kernels, body(): pl.pallas_call(whole, out_shape=(strip, strip, jax.ShapeDtypeStruct((1,),...  78.6 us
    unnamed x10, local copies, waits for them, and re-layouts  4.39 us

profile of v2, /device:TPU:1, one launch (start us, length us, event | category | flops | bytes accessed | tf_op | source)
XLA Modules:
  0.0 90.2 jit_solution(8192582333176865627)
XLA Ops:
  1.3 0.0 copy-start.2
  1.3 0.0 copy-start.3
  2.0 0.0 copy-done.2
  2.0 0.0 copy-done.3
  2.0 0.0 copy-start
  2.0 1.2 %copy-done = f32[1,128,2048]{2,1,0:T(8,128)S(1)} copy-done((f32[1,128,2048]{2,1,0:T(8,128)S(1)}, f32[1,128,2048]{2,1,0:T(8,128)}, u32[]{:S(2)}) %copy-start) | copy-done | bytes 1048600
  3.2 0.0 copy-start.1
  3.2 1.2 %copy-done.1 = f32[1,128,2048]{2,1,0:T(8,128)S(1)} copy-done((f32[1,128,2048]{2,1,0:T(8,128)S(1)}, f32[1,128,2048]{2,1,0:T(8,128)}, u32[]{:S(2)}) %copy-start.1) | copy-done | bytes 1048600
  4.4 78.6 %shard_map.101 = (f32[1,128,2048]{2,1,0:T(8,128)S(1)}, f32[1,128,2048]{2,1,0:T(8,128)S(1)}, s32[1]{0:T(128)}, f32[1]{0:T(128)}, f32[1]{0:T(128)}) custom-call(f32[1,128,2048]{2,1,0:T(8,128)S(1)} %copy-done, f32[1,128,2048]{2,1,0:T(8,128)S(1)} %copy-done.1, s32[1]{0:T(128)S(6)} %copy.16.labels_ref, f32[128]{0:T(128)S(1)} %copy-done.2, s32[1]{0:T(128)S(6)} %copy.17.accept_ref, ...), custom_call_target="tpu_custom_call" | custom-call | tf_op jit(solution)/shard_map/pallas_call | solution.py:336
  83.0 1.0 %copy.18 = f32[1,128,2048]{2,1,0:T(8,128)} copy(f32[1,128,2048]{2,1,0:T(8,128)S(1)} %get-tuple-element.10) | data formatting | bytes 2097152
  84.0 1.0 %copy.19 = f32[1,128,2048]{2,1,0:T(8,128)} copy(f32[1,128,2048]{2,1,0:T(8,128)S(1)} %get-tuple-element.11) | data formatting | bytes 2097152
Async XLA Ops:
  1.3 0.7 copy-start.2
  1.3 0.7 copy-start.3
  2.0 1.2 %copy-start = (f32[1,128,2048]{2,1,0:T(8,128)S(1)}, f32[1,128,2048]{2,1,0:T(8,128)}, u32[]{:S(2)}) copy-start(f32[1,128,2048]{2,1,0:T(8,128)} %field_ref.1) | copy-start | bytes 3145732
  3.2 1.2 %copy-start.1 = (f32[1,128,2048]{2,1,0:T(8,128)S(1)}, f32[1,128,2048]{2,1,0:T(8,128)}, u32[]{:S(2)}) copy-start(f32[1,128,2048]{2,1,0:T(8,128)} %moment_ref.1) | copy-start | bytes 3145732

commit v3 on v2

v3 whole, which is shorter than its diff:
```python
import functools
import jax
import jax.numpy as jnp
from jax import lax
from jax.experimental import pallas as pl
from jax.experimental.pallas import tpu as pltpu
from jax.sharding import PartitionSpec as P

MESH = pl.DeviceIdType.MESH

HOP = 0.36
QUARTIC = 0.3
EPS = 0.05
F32 = jnp.float32
BF16 = jnp.bfloat16

def split_rep(rep):
    return rep // 32, (rep // 4) % 8, (rep // 2) % 2, rep % 2


def join_rep(x, z, y, c):
    return ((x * 8 + z) * 2 + y) * 2 + c


def table_place(rep):
    x, z, y, c = split_rep(rep)
    return ((x * 2 + y) * 2 + c) * 8 + z


def tile_of(ref, chunk, home):
    cols = pl.ds(pl.multiple_of(lax.rem(home, 16) * 128, 128), 128)
    if chunk == 0:
        return ref.at[4 + lax.div(home, 16), :, cols]
    b = lax.div(home, 32)
    block = 2 + b + 8 * lax.div(b, 2) if chunk == 1 else b + 12 * lax.div(b, 2)
    half = pl.ds(pl.multiple_of(4 * lax.rem(lax.div(home, 16), 2), 4), 4)
    return ref.at[block, half, cols]


def wait_for(ref, sem):
    pltpu.make_async_copy(ref, ref, sem).wait()


def rows_of(block):
    return pl.ds(pl.multiple_of(block * 8, 8), 8)


def lateral(q):
    even, odd = q[:, :1024], q[:, 1024:]
    after = pltpu.roll(even, 1023, 1)
    return jnp.concatenate((odd + pltpu.roll(odd, 1, 1), even + after), 1), jnp.concatenate((odd, after), 1)


def fold(v):
    total = v[:, :128]
    for j in range(1, 16):
        total = total + v[:, 128 * j : 128 * j + 128]
    return total


def split_two(v):
    high = v.astype(BF16)
    return high, (v - high.astype(F32)).astype(BF16)


def site(q, below, right):
    squared = q * q
    return -HOP * q * (below + right) + squared + QUARTIC * (squared - 1.0) * (squared - 1.0)


def whole(
    field_hbm, moment_hbm, labels_hbm, betas_hbm, accept_hbm, pairs_hbm,
    out_hbm, sorted_ref, new_hbm, change_hbm, ladder_hbm,
    labels_ref, betas_ref, accept_ref, pairs_ref, new_ref, change_ref, ladder_ref, out_ref,
    field_ref, moment_ref, q0, m0, qa_0, qa_1, pa, qe_0, qe_1, pe, perm, perm_back,
    got_0, got_1, got_2, picked_0, picked_1, picked_2, label_row, label_tab, act_row, act_got, act_sum, act_tab, holder_row, holder_ref,
    send_h, recv_h, send_1, recv_1, send_2, recv_2, send_lab, recv_lab, send_act, recv_act, local_sem, load_sem, small_sem, store_sem,
):
    me = lax.axis_index("rep")
    dom = lax.axis_index("dom")
    other = 1 - dom
    x, z, y, c = split_rep(me)
    place = table_place(me)
    group = lax.div(place, 8)
    got = (got_0, got_1, got_2)
    picked = (picked_0, picked_1, picked_2)

    loads = []
    for k, (src, dst) in enumerate(((field_hbm, field_ref), (moment_hbm, moment_ref))):
        loads.append(pltpu.make_async_copy(src.at[0], dst, load_sem.at[k]))
        loads[k].start()
    small = []
    for k, (src, dst) in enumerate(
        ((labels_hbm, labels_ref), (betas_hbm, betas_ref), (accept_hbm, accept_ref), (pairs_hbm, pairs_ref))
    ):
        small.append(pltpu.make_async_copy(src, dst, small_sem.at[k]))
        small[k].start()

    def push(src, dst, send_sem, recv_sem, rep):
        pltpu.make_async_remote_copy(
            src_ref=src, dst_ref=dst, send_sem=send_sem, recv_sem=recv_sem,
            device_id=(rep, other), device_id_type=MESH,
        ).start()

    barrier = pltpu.get_barrier_semaphore()

    xs = [lax.rem(x + k, 4) * 32 for k in (2, 1, 3, 0)]
    zs = [lax.rem(z + k, 8) * 4 for k in (4, 3, 5, 2, 6, 1, 7, 0)]
    for at_z in zs:
        for at_x in xs:
            for k in range(4):
                pl.semaphore_signal(barrier, inc=1, device_id=(at_x + at_z + k, other), device_id_type=MESH)

    for copy in small:
        copy.wait()
    label = labels_ref[0]
    coldness = betas_ref[label]
    new_label = pairs_ref[label]
    accepted = accept_ref[0] == 1
    new_ref[0] = new_label
    stores = [pltpu.make_async_copy(new_ref, new_hbm, store_sem.at[0])]
    stores[0].start()
    label_row[...] = jnp.full((1, 128), new_label, jnp.int32)

    i0 = lax.broadcasted_iota(jnp.int32, (256, 256), 0)
    i1 = lax.broadcasted_iota(jnp.int32, (256, 256), 1)
    there = jnp.where(i1 < 128, 2 * i1, 2 * i1 - 255) == i0
    back = jnp.where(i0 < 128, 2 * i0, 2 * i0 - 255) == i1
    for third in range(3):
        perm[pl.ds(256 * third, 256), :] = jnp.where(there, 1.0, 0.0).astype(BF16)
    for half in range(2):
        perm_back[pl.ds(256 * half, 256), :] = jnp.where(back, 1.0, 0.0).astype(BF16)

    def apart(ref, dst, r):
        values = ref[pl.ds(pl.multiple_of(32 * r, 32), 32), :]
        high = values.astype(BF16)
        pieces = (high, *split_two(values - high.astype(F32)))
        cols = [slice(256 * b, 256 * b + 256) for b in range(8)]
        left = jnp.concatenate([jnp.concatenate([v[:, s] for v in pieces], 1) for s in cols], 0)
        res = jnp.dot(left, perm[...], preferred_element_type=F32)
        rows = pl.ds(pl.multiple_of(16 + 32 * r, 16), 32)
        for b in range(8):
            dst[rows, 128 * b : 128 * b + 128] = res[32 * b : 32 * b + 32, :128]
            dst[rows, 1024 + 128 * b : 1152 + 128 * b] = res[32 * b : 32 * b + 32, 128:]

    def joined(values):
        high, low = split_two(values)
        parts = []
        for b in range(8):
            e = slice(128 * b, 128 * b + 128)
            o = slice(1024 + 128 * b, 1152 + 128 * b)
            parts.append(jnp.concatenate((high[:, e], high[:, o], low[:, e], low[:, o]), 1))
        res = jnp.dot(jnp.concatenate(parts, 0), perm_back[...], preferred_element_type=F32)
        return jnp.concatenate([res[32 * b : 32 * b + 32] for b in range(8)], 1)

    def settle(values, rows):
        for at, n, first in rows:
            new = jnp.where(accepted, values[at : at + n], field_ref[pl.ds(first, n), :])
            out_ref[pl.ds(first // 8, n // 8)] = new.reshape(n // 8, 8, 2048)

    for load, ref, dst in zip(loads, (field_ref, moment_ref), (q0, m0)):
        load.wait()

        def set_apart(r, carry, ref=ref, dst=dst):
            apart(ref, dst, r)
            return carry

        lax.fori_loop(0, 4, set_apart, 0)

    row = lax.broadcasted_iota(jnp.int32, (8, 2048), 0)
    a = coldness * (EPS * HOP)
    b = coldness * (EPS * (2.0 - 4.0 * QUARTIC))
    g = coldness * (EPS * 4.0 * QUARTIC)

    def around(ref, block):
        q = ref[rows_of(block), :]
        above = pltpu.roll(jnp.where(row == 7, ref[rows_of(block - 1), :], q), 1, 0)
        below = pltpu.roll(jnp.where(row == 0, ref[rows_of(block + 1), :], q), 7, 0)
        return q, above, below

    def kicked(q, above, below, beside, moment, share):
        near = (above + below) + beside
        return moment + (near * (share * a) - q * (q * q * (share * g) + share * b))

    def leap(src, src_at, mom, mom_at, dst, dst_p, at, first):
        q, above, below = around(src, src_at)
        beside, _ = lateral(q)
        moment = mom[rows_of(mom_at), :]
        moment = kicked(q, above, below, beside, moment, 0.5 if first else 1.0)
        dst_p[rows_of(at), :] = moment
        dst[rows_of(at), :] = q + EPS * moment

    def finish(src, src_at, mom, mom_at, start_at, sums):
        q, above, below = around(src, src_at)
        beside, right = lateral(q)
        moment = kicked(q, above, below, beside, mom[rows_of(mom_at), :], 0.5)
        new = site(q, below, right)
        p, _, p_below = around(q0, start_at)
        old = site(p, p_below, lateral(p)[1])
        start = m0[rows_of(start_at), :]
        change = (0.5 * moment * moment + coldness * new) - (0.5 * start * start + coldness * old)
        return sums[0] + fold(change), sums[1] + fold(jnp.where(accepted, new, old))

    def inner(src, dst, mom, first):
        def some(n, carry):
            for k in range(7):
                at = 3 + 7 * n + k
                leap(src, at, mom, at, dst, pa, at, first)
            return carry

        lax.fori_loop(0, 2, some, 0)

    def inner_pair(n, carry):
        inner(qa_0, qa_1, pa, False)
        inner(qa_1, qa_0, pa, False)
        return carry

    inner(q0, qa_0, m0, True)
    lax.fori_loop(0, 3, inner_pair, 0)
    inner(qa_0, qa_1, pa, False)
    zero = jnp.zeros((8, 128), F32)
    for part in range(2):
        first = 32 + 32 * part
        settle(joined(qa_1[pl.ds(16 + first, 32), :]), [(0, 32, first)])

    def to_column(src, tab, send_sem, recv_sem):
        for k in range(8):
            push(src, tab.at[place], send_sem, recv_sem, join_rep(x, (z + k) % 8, y, c))

    def to_plane(tab, dst, send_sem, recv_sem):
        block = pl.ds(pl.multiple_of(group * 8, 8), 8)
        for k in range(16):
            push(
                tab.at[block], dst.at[block], send_sem, recv_sem,
                join_rep((x + k // 4) % 4, z, (y + (k // 2) % 2) % 2, (c + k % 2) % 2),
            )

    def spread(chunk, first=0, last=128):
        def one(k, carry):
            home = lax.rem(me + k, 128)
            push(tile_of(out_ref, chunk, home), got[chunk].at[me], send_1.at[chunk], recv_1.at[chunk], home)
            return carry

        lax.fori_loop(first, last, one, 0, unroll=4)

    def pick(chunk):
        def one(t, carry):
            picked[chunk][t] = got[chunk][holder_ref[0, t]]
            return carry

        lax.fori_loop(0, 128, one, 0, unroll=8)

    def give(chunk):
        def one(k, carry):
            goal = lax.rem(me + k, 128)
            push(picked[chunk].at[goal], tile_of(sorted_ref, chunk, me), send_2.at[chunk], recv_2, goal)
            return carry

        lax.fori_loop(0, 128, one, 0, unroll=4)

    halos = ((q0, 136, 8), (q0, 16, 144), (m0, 136, 8), (m0, 16, 144))
    edges = ((q0, 135, 7), (q0, 24, 152))

    def halo(k, n):
        ref, src_row, dst_row = halos[k]
        cols = pl.ds(pl.multiple_of(256 * n, 128), 256)
        push(
            ref.at[pl.ds(src_row, 8), cols], ref.at[pl.ds(dst_row, 8), cols],
            send_h.at[k], recv_h.at[k], me,
        )

    pl.semaphore_wait(barrier, 128)
    to_column(label_row, label_tab.at[0], send_lab.at[0], recv_lab.at[0])
    for k, (ref, src_row, dst_row) in enumerate(edges):
        push(ref.at[pl.ds(src_row, 1)], ref.at[pl.ds(dst_row, 1)], send_h.at[4 + k], recv_h.at[4 + k], me)

    def spread_and_halo(n, carry):
        for k in range(4):
            halo(k, n)
            for at in range(4):
                home = lax.rem(me + 16 * n + 4 * k + at, 128)
                push(tile_of(out_ref, 0, home), got_0.at[me], send_1.at[0], recv_1.at[0], home)
        return carry

    lax.fori_loop(0, 4, spread_and_halo, 0)
    wait_for(label_tab.at[0, pl.ds(0, 8)], recv_lab.at[0])
    to_plane(label_tab.at[0], label_tab.at[1], send_lab.at[1], recv_lab.at[1])
    lax.fori_loop(4, 8, spread_and_halo, 0)
    settle(
        joined(jnp.concatenate((qa_1[pl.ds(32, 16), :], qa_1[pl.ds(112, 16), :]), 0)),
        [(0, 16, 16), (16, 16, 96)],
    )
    spread(1)

    def inner_last(i, sums):
        return finish(qa_1, i, pa, i, i, sums)

    sums = lax.fori_loop(4, 16, inner_last, (zero, zero))

    lane = lax.broadcasted_iota(jnp.int32, (1, 128), 1)
    wait_for(label_tab.at[1], recv_lab.at[1])
    holder = jnp.zeros((1, 128), jnp.int32)
    for p in range(128):
        rep = join_rep(p // 32, p % 8, (p // 16) % 2, (p // 8) % 2)
        holder = jnp.maximum(holder, jnp.where(label_tab[1, p] == lane, rep, 0))
    holder_row[...] = holder
    copy = pltpu.make_async_copy(holder_row, holder_ref, local_sem)
    copy.start()
    copy.wait()

    wait_for(got_0, recv_1.at[0])
    pick(0)
    give(0)

    for k, (ref, src_row, dst_row) in enumerate(halos):
        wait_for(ref.at[pl.ds(dst_row, 8)], recv_h.at[k])
    for k, (ref, src_row, dst_row) in enumerate(edges):
        wait_for(ref.at[pl.ds(dst_row, 1)], recv_h.at[4 + k])

    def outer(src, dst, mom, first):
        def some(side, carry):
            for k in range(1, 5):
                at = (14 if first else 6) * side + k
                leap(src, at, mom, at, dst, pe, 6 * side + k, first)
            return carry

        lax.fori_loop(0, 2, some, 0)

    def outer_pair(n, carry):
        outer(qe_0, qe_1, pe, False)
        outer(qe_1, qe_0, pe, False)
        return carry

    outer(q0, qe_0, m0, True)
    lax.fori_loop(0, 3, outer_pair, 0)
    outer(qe_0, qe_1, pe, False)
    settle(
        joined(jnp.concatenate((qe_1[pl.ds(16, 16), :], qe_1[pl.ds(64, 16), :]), 0)),
        [(0, 16, 0), (16, 16, 112)],
    )
    spread(2)
    stores.append(pltpu.make_async_copy(out_ref, out_hbm, store_sem.at[1]))
    stores[1].start()

    def outer_last(i, sums):
        side, local = lax.div(i, 2), 2 + lax.rem(i, 2)
        return finish(qe_1, 6 * side + local, pe, 6 * side + local, 14 * side + local, sums)

    sums = lax.fori_loop(0, 4, outer_last, sums)
    act_row[...] = jnp.where(lane == 0, jnp.sum(sums[1]), jnp.where(lane == 1, jnp.sum(sums[0]), 0.0))
    push(act_row, act_got, send_act.at[0], recv_act.at[0], me)

    wait_for(got_1, recv_1.at[1])
    pick(1)
    give(1)
    wait_for(act_got, recv_act.at[0])
    total = act_row[...] + act_got[...]
    act_sum[...] = total
    to_column(act_sum, act_tab.at[0], send_act.at[1], recv_act.at[1])
    wait_for(got_2, recv_1.at[2])
    pick(2)
    wait_for(act_tab.at[0, pl.ds(0, 8)], recv_act.at[1])
    to_plane(act_tab.at[0], act_tab.at[1], send_act.at[2], recv_act.at[2])
    give(2)

    for k, (ref, src_row, dst_row) in enumerate(halos):
        wait_for(ref.at[pl.ds(src_row, 8)], send_h.at[k])
    for k, (ref, src_row, dst_row) in enumerate(edges):
        wait_for(ref.at[pl.ds(src_row, 1)], send_h.at[4 + k])
    wait_for(label_tab.at[0, pl.ds(0, 8)], send_lab.at[0])
    wait_for(label_tab.at[1], send_lab.at[1])
    wait_for(act_got, send_act.at[0])
    wait_for(act_tab.at[0, pl.ds(0, 8)], send_act.at[1])
    for chunk in range(3):
        wait_for(got[chunk], send_1.at[chunk])
    change_ref[0] = jnp.sum(jnp.where(lane == 1, total, 0.0))
    stores.append(pltpu.make_async_copy(change_ref, change_hbm, store_sem.at[2]))
    stores[2].start()
    wait_for(act_tab.at[1], recv_act.at[2])
    ladder = jnp.zeros((1, 128), F32)
    for p in range(128):
        ladder = ladder + jnp.where(label_tab[1, p] == me, act_tab[1, p], 0.0)
    ladder_ref[0] = jnp.sum(jnp.where(lane == 0, ladder, 0.0)) / 524288.0
    stores.append(pltpu.make_async_copy(ladder_ref, ladder_hbm, store_sem.at[3]))
    stores[3].start()
    for copy in stores:
        copy.wait()
    wait_for(act_tab.at[1], send_act.at[2])
    for chunk in range(3):
        wait_for(got[chunk], send_2.at[chunk])
    wait_for(sorted_ref, recv_2)


def hand_over(*refs):
    given, results, held, load_sem, store_sem, small_sem = refs[:5], refs[5:10], refs[10], refs[11], refs[12], refs[13]
    small = [pltpu.make_async_copy(given[k], results[k], small_sem.at[k - 2]) for k in range(2, 5)]
    for copy in small:
        copy.start()
    loads, stores = [], []
    for k in range(2):
        for n in range(4):
            part = pl.ds(4 * n, 4)
            loads.append(pltpu.make_async_copy(given[k].at[part], held.at[k, part], load_sem.at[4 * k + n]))
            stores.append(pltpu.make_async_copy(held.at[k, part], results[k].at[part], store_sem.at[4 * k + n]))
    for copy in loads:
        copy.start()
    for load, store in zip(loads, stores):
        load.wait()
        store.start()
    for copy in stores + small:
        copy.wait()


def body(field, momentum, labels, betas, accept, swap_pairs):
    i32 = jnp.int32
    dma = pltpu.SemaphoreType.DMA
    strip = jax.ShapeDtypeStruct((16, 8, 2048), F32)
    hbm = pl.BlockSpec(memory_space=pltpu.HBM)
    shapes = (
        strip, strip, jax.ShapeDtypeStruct((1,), i32),
        jax.ShapeDtypeStruct((1,), F32), jax.ShapeDtypeStruct((1,), F32),
    )
    results = pl.pallas_call(
        whole,
        out_shape=shapes,
        in_specs=[hbm] * 6,
        out_specs=(hbm,) * 5,
        scratch_shapes=[
            pltpu.SMEM((1,), i32),
            pltpu.SMEM((128,), F32),
            pltpu.SMEM((1,), i32),
            pltpu.SMEM((128,), i32),
            pltpu.SMEM((1,), i32),
            pltpu.SMEM((1,), F32),
            pltpu.SMEM((1,), F32),
            pltpu.VMEM((16, 8, 2048), F32),
            pltpu.VMEM((128, 2048), F32),
            pltpu.VMEM((128, 2048), F32),
            pltpu.VMEM((160, 2048), F32),
            pltpu.VMEM((160, 2048), F32),
            pltpu.VMEM((160, 2048), F32),
            pltpu.VMEM((160, 2048), F32),
            pltpu.VMEM((160, 2048), F32),
            pltpu.VMEM((96, 2048), F32),
            pltpu.VMEM((96, 2048), F32),
            pltpu.VMEM((96, 2048), F32),
            pltpu.VMEM((768, 256), BF16),
            pltpu.VMEM((512, 256), BF16),
            pltpu.VMEM((128, 8, 128), F32),
            pltpu.VMEM((128, 4, 128), F32),
            pltpu.VMEM((128, 4, 128), F32),
            pltpu.VMEM((128, 8, 128), F32),
            pltpu.VMEM((128, 4, 128), F32),
            pltpu.VMEM((128, 4, 128), F32),
            pltpu.VMEM((1, 128), i32),
            pltpu.VMEM((2, 128, 1, 128), i32),
            pltpu.VMEM((1, 128), F32),
            pltpu.VMEM((1, 128), F32),
            pltpu.VMEM((1, 128), F32),
            pltpu.VMEM((2, 128, 1, 128), F32),
            pltpu.VMEM((1, 128), i32),
            pltpu.SMEM((1, 128), i32),
            dma((6,)), dma((6,)), dma((3,)), dma((3,)), dma((3,)), dma(()),
            dma((2,)), dma((2,)), dma((3,)), dma((3,)), dma(()), dma((2,)), dma((4,)), dma((4,)),
        ],
        compiler_params=pltpu.CompilerParams(collective_id=0, has_side_effects=True, vmem_limit_bytes=67_000_000),
    )(field, momentum, labels, betas, accept, swap_pairs)
    out, ordered, new_label, change, ladder = pl.pallas_call(
        hand_over,
        out_shape=shapes,
        in_specs=[hbm] * 5,
        out_specs=(hbm,) * 5,
        scratch_shapes=[pltpu.VMEM((2, 16, 8, 2048), F32), dma((8,)), dma((8,)), dma((3,))],
        compiler_params=pltpu.CompilerParams(vmem_limit_bytes=67_000_000),
    )(*results)
    return out.reshape(1, 128, 2048), ordered.reshape(1, 128, 2048), new_label, change, ladder


def solution(mesh):
    rep = P("rep")
    strip = P("rep", "dom", None)
    in_specs = (strip, strip, rep, P(), rep, P())
    out_specs = (strip, strip, rep, rep, rep)
    return jax.shard_map(body, mesh=mesh, in_specs=in_specs, out_specs=out_specs, check_vma=False)
```

time: 90.4 us -> 75.7 us (0.84)
  between operations: 7.24 us -> 1.93 us
  Pallas kernels: 78.6 us -> 73.6 us
  local copies, waits for them, and re-layouts: 4.39 us -> 0 us
    pallas_call x1 -> x2, Pallas kernels: 78.6 us -> 73.6 us  [the longest x1 69.4 us: body(): pl.pallas_call(whole, out_shape=shapes, in_specs=[hbm] * 6, out_specs=(hb...]
    unnamed x10 -> x0, local copies, waits for them, and re-layouts: 4.39 us -> none
where the time goes in v3:
time: 75.7 us; the launch traced here: 75.5 us
  Pallas kernels  73.6 us (97%)
  between operations  1.93 us (3%)
    pallas_call x1, Pallas kernels, body(): pl.pallas_call(whole, out_shape=shapes, in_specs=[hbm] * 6, out_specs=(hb...  69.4 us
    pallas_call x1, Pallas kernels, body(): pl.pallas_call(hand_over, out_shape=shapes, in_specs=[hbm] * 5, out_specs...  4.21 us

profile of v3, /device:TPU:1, one launch (start us, length us, event | category | flops | bytes accessed | tf_op | source)
XLA Modules:
  0.0 75.5 jit_solution(12245456243292030398)
XLA Ops:
  1.9 69.4 %shard_map.101 = (f32[16,8,2048]{2,1,0:T(8,128)}, f32[16,8,2048]{2,1,0:T(8,128)}, s32[1]{0:T(128)}, f32[1]{0:T(128)}, f32[1]{0:T(128)}) custom-call(f32[1,128,2048]{2,1,0:T(8,128)} %field_hbm.1, f32[1,128,2048]{2,1,0:T(8,128)} %moment_hbm.1, s32[1]{0:T(128)S(6)} %copy.11.labels_hbm, f32[128]{0:T(128)} %betas_hbm.1, s32[1]{0:T(128)S(6)} %copy.12.accept_hbm, ...), custom_call_target="tpu_custom_call" | custom-call | tf_op jit(solution)/shard_map/pallas_call | solution.py:423
  71.3 4.2 %shard_map.102 = (f32[16,8,2048]{2,1,0:T(8,128)}, f32[16,8,2048]{2,1,0:T(8,128)}, s32[1]{0:T(128)}, f32[1]{0:T(128)}, f32[1]{0:T(128)}) custom-call(f32[16,8,2048]{2,1,0:T(8,128)} %get-tuple-element.15.refs_0_, f32[16,8,2048]{2,1,0:T(8,128)} %get-tuple-element.16.refs_1_, s32[1]{0:T(128)} %get-tuple-element.17.refs_2_, f32[1]{0:T(128)} %get-tuple-element.18.refs_3_, ...), custom_call_target="tpu_custom_call" | custom-call | tf_op jit(solution)/shard_map/pallas_call | solution.py:468

commit v4 on v3

--- a/solution.py
+++ b/solution.py
@@ -29,10 +29,11 @@
 
 def tile_of(ref, chunk, home):
     cols = pl.ds(pl.multiple_of(lax.rem(home, 16) * 128, 128), 128)
-    if chunk == 0:
-        return ref.at[4 + lax.div(home, 16), :, cols]
+    if chunk == 1:
+        b = lax.div(home, 16)
+        return ref.at[2 + b + 4 * lax.div(b, 4), :, cols]
     b = lax.div(home, 32)
-    block = 2 + b + 8 * lax.div(b, 2) if chunk == 1 else b + 12 * lax.div(b, 2)
+    block = 6 + b if chunk == 0 else b + 12 * lax.div(b, 2)
     half = pl.ds(pl.multiple_of(4 * lax.rem(lax.div(home, 16), 2), 4), 4)
     return ref.at[block, half, cols]
 
@@ -70,8 +71,8 @@
 
 def whole(
     field_hbm, moment_hbm, labels_hbm, betas_hbm, accept_hbm, pairs_hbm,
-    out_hbm, sorted_ref, new_hbm, change_hbm, ladder_hbm,
-    labels_ref, betas_ref, accept_ref, pairs_ref, new_ref, change_ref, ladder_ref, out_ref,
+    out_ref, sorted_ref, new_hbm, change_hbm, ladder_hbm,
+    labels_ref, betas_ref, accept_ref, pairs_ref, new_ref, change_ref, ladder_ref,
     field_ref, moment_ref, q0, m0, qa_0, qa_1, pa, qe_0, qe_1, pe, perm, perm_back,
     got_0, got_1, got_2, picked_0, picked_1, picked_2, label_row, label_tab, act_row, act_got, act_sum, act_tab, holder_row, holder_ref,
     send_h, recv_h, send_1, recv_1, send_2, recv_2, send_lab, recv_lab, send_act, recv_act, local_sem, load_sem, small_sem, store_sem,
@@ -86,9 +87,11 @@
     picked = (picked_0, picked_1, picked_2)
 
     loads = []
-    for k, (src, dst) in enumerate(((field_hbm, field_ref), (moment_hbm, moment_ref))):
-        loads.append(pltpu.make_async_copy(src.at[0], dst, load_sem.at[k]))
-        loads[k].start()
+    for first, n in ((32, 64), (0, 32), (96, 32)):
+        rows = pl.ds(first, n)
+        for src, dst in ((field_hbm, field_ref), (moment_hbm, moment_ref)):
+            loads.append(pltpu.make_async_copy(src.at[0, rows], dst.at[rows], load_sem.at[len(loads)]))
+            loads[-1].start()
     small = []
     for k, (src, dst) in enumerate(
         ((labels_hbm, labels_ref), (betas_hbm, betas_ref), (accept_hbm, accept_ref), (pairs_hbm, pairs_ref))
@@ -158,14 +161,17 @@
             new = jnp.where(accepted, values[at : at + n], field_ref[pl.ds(first, n), :])
             out_ref[pl.ds(first // 8, n // 8)] = new.reshape(n // 8, 8, 2048)
 
-    for load, ref, dst in zip(loads, (field_ref, moment_ref), (q0, m0)):
-        load.wait()
-
-        def set_apart(r, carry, ref=ref, dst=dst):
-            apart(ref, dst, r)
-            return carry
-
-        lax.fori_loop(0, 4, set_apart, 0)
+    def set_apart(first, stride):
+        def one(n, carry):
+            apart(field_ref, q0, first + stride * n)
+            apart(moment_ref, m0, first + stride * n)
+            return carry
+
+        lax.fori_loop(0, 2, one, 0)
+
+    loads[0].wait()
+    loads[1].wait()
+    set_apart(1, 1)
 
     row = lax.broadcasted_iota(jnp.int32, (8, 2048), 0)
     a = coldness * (EPS * HOP)
@@ -201,27 +207,30 @@
         change = (0.5 * moment * moment + coldness * new) - (0.5 * start * start + coldness * old)
         return sums[0] + fold(change), sums[1] + fold(jnp.where(accepted, new, old))
 
-    def inner(src, dst, mom, first):
-        def some(n, carry):
-            for k in range(7):
-                at = 3 + 7 * n + k
-                leap(src, at, mom, at, dst, pa, at, first)
-            return carry
-
-        lax.fori_loop(0, 2, some, 0)
-
-    def inner_pair(n, carry):
-        inner(qa_0, qa_1, pa, False)
-        inner(qa_1, qa_0, pa, False)
-        return carry
-
-    inner(q0, qa_0, m0, True)
-    lax.fori_loop(0, 3, inner_pair, 0)
-    inner(qa_0, qa_1, pa, False)
-    zero = jnp.zeros((8, 128), F32)
-    for part in range(2):
-        first = 32 + 32 * part
-        settle(joined(qa_1[pl.ds(16 + first, 32), :]), [(0, 32, first)])
+    def inner(base, count):
+        def sweep(src, dst, mom, first):
+            def some(n, carry):
+                for k in range(6):
+                    at = base + 8 * n + k
+                    leap(src, at, mom, at, dst, pa, at, first)
+                return carry
+
+            lax.fori_loop(0, count, some, 0)
+
+        def pair(n, carry):
+            sweep(qa_0, qa_1, pa, False)
+            sweep(qa_1, qa_0, pa, False)
+            return carry
+
+        sweep(q0, qa_0, m0, True)
+        lax.fori_loop(0, 3, pair, 0)
+        sweep(qa_0, qa_1, pa, False)
+
+    def inner_last(first, last, sums):
+        return lax.fori_loop(first, last, lambda i, sums: finish(qa_1, i, pa, i, i, sums), sums)
+
+    inner(7, 1)
+    settle(joined(qa_1[pl.ds(64, 32), :]), [(0, 32, 48)])
 
     def to_column(src, tab, send_sem, recv_sem):
         for k in range(8):
@@ -271,6 +280,18 @@
 
     pl.semaphore_wait(barrier, 128)
     to_column(label_row, label_tab.at[0], send_lab.at[0], recv_lab.at[0])
+    spread(0)
+    zero = jnp.zeros((8, 128), F32)
+    sums = inner_last(8, 12, (zero, zero))
+    for load in loads[2:]:
+        load.wait()
+    set_apart(0, 3)
+    wait_for(label_tab.at[0, pl.ds(0, 8)], recv_lab.at[0])
+    to_plane(label_tab.at[0], label_tab.at[1], send_lab.at[1], recv_lab.at[1])
+    inner(3, 2)
+    for part in range(2):
+        settle(joined(qa_1[pl.ds(32 + 64 * part, 32), :]), [(0, 32, 16 + 64 * part)])
+
     for k, (ref, src_row, dst_row) in enumerate(edges):
         push(ref.at[pl.ds(src_row, 1)], ref.at[pl.ds(dst_row, 1)], send_h.at[4 + k], recv_h.at[4 + k], me)
 
@@ -279,23 +300,10 @@
             halo(k, n)
             for at in range(4):
                 home = lax.rem(me + 16 * n + 4 * k + at, 128)
-                push(tile_of(out_ref, 0, home), got_0.at[me], send_1.at[0], recv_1.at[0], home)
+                push(tile_of(out_ref, 1, home), got_1.at[me], send_1.at[1], recv_1.at[1], home)
         return carry
 
-    lax.fori_loop(0, 4, spread_and_halo, 0)
-    wait_for(label_tab.at[0, pl.ds(0, 8)], recv_lab.at[0])
-    to_plane(label_tab.at[0], label_tab.at[1], send_lab.at[1], recv_lab.at[1])
-    lax.fori_loop(4, 8, spread_and_halo, 0)
-    settle(
-        joined(jnp.concatenate((qa_1[pl.ds(32, 16), :], qa_1[pl.ds(112, 16), :]), 0)),
-        [(0, 16, 16), (16, 16, 96)],
-    )
-    spread(1)
-
-    def inner_last(i, sums):
-        return finish(qa_1, i, pa, i, i, sums)
-
-    sums = lax.fori_loop(4, 16, inner_last, (zero, zero))
+    lax.fori_loop(0, 8, spread_and_halo, 0)
 
     lane = lax.broadcasted_iota(jnp.int32, (1, 128), 1)
     wait_for(label_tab.at[1], recv_lab.at[1])
@@ -311,6 +319,8 @@
     wait_for(got_0, recv_1.at[0])
     pick(0)
     give(0)
+    sums = inner_last(4, 8, sums)
+    sums = inner_last(12, 16, sums)
 
     for k, (ref, src_row, dst_row) in enumerate(halos):
         wait_for(ref.at[pl.ds(dst_row, 8)], recv_h.at[k])
@@ -339,8 +349,6 @@
         [(0, 16, 0), (16, 16, 112)],
     )
     spread(2)
-    stores.append(pltpu.make_async_copy(out_ref, out_hbm, store_sem.at[1]))
-    stores[1].start()
 
     def outer_last(i, sums):
         side, local = lax.div(i, 2), 2 + lax.rem(i, 2)
@@ -374,15 +382,15 @@
     for chunk in range(3):
         wait_for(got[chunk], send_1.at[chunk])
     change_ref[0] = jnp.sum(jnp.where(lane == 1, total, 0.0))
-    stores.append(pltpu.make_async_copy(change_ref, change_hbm, store_sem.at[2]))
-    stores[2].start()
+    stores.append(pltpu.make_async_copy(change_ref, change_hbm, store_sem.at[1]))
+    stores[1].start()
     wait_for(act_tab.at[1], recv_act.at[2])
     ladder = jnp.zeros((1, 128), F32)
     for p in range(128):
         ladder = ladder + jnp.where(label_tab[1, p] == me, act_tab[1, p], 0.0)
     ladder_ref[0] = jnp.sum(jnp.where(lane == 0, ladder, 0.0)) / 524288.0
-    stores.append(pltpu.make_async_copy(ladder_ref, ladder_hbm, store_sem.at[3]))
-    stores[3].start()
+    stores.append(pltpu.make_async_copy(ladder_ref, ladder_hbm, store_sem.at[2]))
+    stores[2].start()
     for copy in stores:
         copy.wait()
     wait_for(act_tab.at[1], send_act.at[2])
@@ -391,23 +399,12 @@
     wait_for(sorted_ref, recv_2)
 
 
-def hand_over(*refs):
-    given, results, held, load_sem, store_sem, small_sem = refs[:5], refs[5:10], refs[10], refs[11], refs[12], refs[13]
-    small = [pltpu.make_async_copy(given[k], results[k], small_sem.at[k - 2]) for k in range(2, 5)]
-    for copy in small:
+def hand_over(out_in, sorted_in, new_in, change_in, ladder_in, out, ordered, new, change, ladder, sems):
+    pairs = ((out_in, out), (sorted_in, ordered), (new_in, new), (change_in, change), (ladder_in, ladder))
+    copies = [pltpu.make_async_copy(src, dst, sems.at[k]) for k, (src, dst) in enumerate(pairs)]
+    for copy in copies:
         copy.start()
-    loads, stores = [], []
-    for k in range(2):
-        for n in range(4):
-            part = pl.ds(4 * n, 4)
-            loads.append(pltpu.make_async_copy(given[k].at[part], held.at[k, part], load_sem.at[4 * k + n]))
-            stores.append(pltpu.make_async_copy(held.at[k, part], results[k].at[part], store_sem.at[4 * k + n]))
-    for copy in loads:
-        copy.start()
-    for load, store in zip(loads, stores):
-        load.wait()
-        store.start()
-    for copy in stores + small:
+    for copy in copies:
         copy.wait()
 
 
@@ -416,6 +413,7 @@
     dma = pltpu.SemaphoreType.DMA
     strip = jax.ShapeDtypeStruct((16, 8, 2048), F32)
     hbm = pl.BlockSpec(memory_space=pltpu.HBM)
+    vmem = pl.BlockSpec(memory_space=pltpu.VMEM)
     shapes = (
         strip, strip, jax.ShapeDtypeStruct((1,), i32),
         jax.ShapeDtypeStruct((1,), F32), jax.ShapeDtypeStruct((1,), F32),
@@ -424,7 +422,7 @@
         whole,
         out_shape=shapes,
         in_specs=[hbm] * 6,
-        out_specs=(hbm,) * 5,
+        out_specs=(vmem, vmem, hbm, hbm, hbm),
         scratch_shapes=[
             pltpu.SMEM((1,), i32),
             pltpu.SMEM((128,), F32),
@@ -433,7 +431,6 @@
             pltpu.SMEM((1,), i32),
             pltpu.SMEM((1,), F32),
             pltpu.SMEM((1,), F32),
-            pltpu.VMEM((16, 8, 2048), F32),
             pltpu.VMEM((128, 2048), F32),
             pltpu.VMEM((128, 2048), F32),
             pltpu.VMEM((160, 2048), F32),
@@ -446,11 +443,11 @@
             pltpu.VMEM((96, 2048), F32),
             pltpu.VMEM((768, 256), BF16),
             pltpu.VMEM((512, 256), BF16),
+            pltpu.VMEM((128, 4, 128), F32),
             pltpu.VMEM((128, 8, 128), F32),
             pltpu.VMEM((128, 4, 128), F32),
             pltpu.VMEM((128, 4, 128), F32),
             pltpu.VMEM((128, 8, 128), F32),
-            pltpu.VMEM((128, 4, 128), F32),
             pltpu.VMEM((128, 4, 128), F32),
             pltpu.VMEM((1, 128), i32),
             pltpu.VMEM((2, 128, 1, 128), i32),
@@ -461,17 +458,17 @@
             pltpu.VMEM((1, 128), i32),
             pltpu.SMEM((1, 128), i32),
             dma((6,)), dma((6,)), dma((3,)), dma((3,)), dma((3,)), dma(()),
-            dma((2,)), dma((2,)), dma((3,)), dma((3,)), dma(()), dma((2,)), dma((4,)), dma((4,)),
+            dma((2,)), dma((2,)), dma((3,)), dma((3,)), dma(()), dma((6,)), dma((4,)), dma((3,)),
         ],
-        compiler_params=pltpu.CompilerParams(collective_id=0, has_side_effects=True, vmem_limit_bytes=67_000_000),
+        compiler_params=pltpu.CompilerParams(collective_id=0, has_side_effects=True, vmem_limit_bytes=53_500_000),
     )(field, momentum, labels, betas, accept, swap_pairs)
     out, ordered, new_label, change, ladder = pl.pallas_call(
         hand_over,
         out_shape=shapes,
-        in_specs=[hbm] * 5,
+        in_specs=[vmem, vmem, hbm, hbm, hbm],
         out_specs=(hbm,) * 5,
-        scratch_shapes=[pltpu.VMEM((2, 16, 8, 2048), F32), dma((8,)), dma((8,)), dma((3,))],
-        compiler_params=pltpu.CompilerParams(vmem_limit_bytes=67_000_000),
+        scratch_shapes=[dma((5,))],
+        compiler_params=pltpu.CompilerParams(vmem_limit_bytes=8 << 20),
     )(*results)
     return out.reshape(1, 128, 2048), ordered.reshape(1, 128, 2048), new_label, change, ladder
 

time: 75.7 us -> 72.8 us (0.962)
  Pallas kernels: 73.6 us -> 70.6 us
    pallas_call x2, Pallas kernels: 73.6 us -> 70.6 us  [the longest x1 67.5 us: body(): pl.pallas_call(whole, out_shape=shapes, in_specs=[hbm] * 6, out_specs=(vm...]
where the time goes in v4:
time: 72.8 us; the launch traced here: 72.6 us
  Pallas kernels  70.6 us (97%)
  between operations  1.98 us (3%)
    pallas_call x1, Pallas kernels, body(): pl.pallas_call(whole, out_shape=shapes, in_specs=[hbm] * 6, out_specs=(vm...  67.5 us
    pallas_call x1, Pallas kernels, body(): pl.pallas_call(hand_over, out_shape=shapes, in_specs=[vmem, vmem, hbm, hb...  3.14 us

profile of v4, /device:TPU:1, one launch (start us, length us, event | category | flops | bytes accessed | tf_op | source)
XLA Modules:
  0.0 72.6 jit_solution(4780109091292485763)
XLA Ops:
  1.3 0.0 copy-start
  1.3 0.0 copy-start.1
  2.0 0.0 copy-done
  2.0 0.0 copy-done.1
  2.0 67.5 %shard_map.101 = (f32[16,8,2048]{2,1,0:T(8,128)S(1)}, f32[16,8,2048]{2,1,0:T(8,128)S(1)}, s32[1]{0:T(128)}, f32[1]{0:T(128)}, f32[1]{0:T(128)}) custom-call(f32[1,128,2048]{2,1,0:T(8,128)} %field_hbm.1, f32[1,128,2048]{2,1,0:T(8,128)} %moment_hbm.1, s32[1]{0:T(128)S(6)} %copy.11.labels_hbm, f32[128]{0:T(128)S(1)} %copy-done, s32[1]{0:T(128)S(6)} %copy.12.accept_hbm, ...), custom_call_target="tpu_custom_call" | custom-call | tf_op jit(solution)/shard_map/pallas_call | solution.py:421
  69.5 3.1 %shard_map.102 = (f32[16,8,2048]{2,1,0:T(8,128)}, f32[16,8,2048]{2,1,0:T(8,128)}, s32[1]{0:T(128)}, f32[1]{0:T(128)}, f32[1]{0:T(128)}) custom-call(f32[16,8,2048]{2,1,0:T(8,128)S(1)} %get-tuple-element.15.out_in, f32[16,8,2048]{2,1,0:T(8,128)S(1)} %get-tuple-element.16.sorted_in, s32[1]{0:T(128)} %get-tuple-element.17.new_in, ...), custom_call_target="tpu_custom_call" | custom-call | tf_op jit(solution)/shard_map/pallas_call | solution.py:465
Async XLA Ops:
  1.3 0.7 copy-start
  1.3 0.7 copy-start.1

commit v5 on v4

--- a/solution.py
+++ b/solution.py
@@ -27,15 +27,10 @@
     return ((x * 2 + y) * 2 + c) * 8 + z
 
 
-def tile_of(ref, chunk, home):
-    cols = pl.ds(pl.multiple_of(lax.rem(home, 16) * 128, 128), 128)
-    if chunk == 1:
-        b = lax.div(home, 16)
-        return ref.at[2 + b + 4 * lax.div(b, 4), :, cols]
-    b = lax.div(home, 32)
-    block = 6 + b if chunk == 0 else b + 12 * lax.div(b, 2)
-    half = pl.ds(pl.multiple_of(4 * lax.rem(lax.div(home, 16), 2), 4), 4)
-    return ref.at[block, half, cols]
+def half_tile(ref, chunk, part, at):
+    b, half = lax.div(part, 2), pl.ds(pl.multiple_of(4 * lax.rem(part, 2), 4), 4)
+    block = b + 12 * lax.div(b, 2) if chunk == 3 else (6, 2, 10)[chunk] + b
+    return ref.at[block, half, pl.ds(pl.multiple_of(128 * at, 128), 128)]
 
 
 def wait_for(ref, sem):
@@ -69,13 +64,16 @@
     return -HOP * q * (below + right) + squared + QUARTIC * (squared - 1.0) * (squared - 1.0)
 
 
+CHUNKS = 4
+
+
 def whole(
     field_hbm, moment_hbm, labels_hbm, betas_hbm, accept_hbm, pairs_hbm,
-    out_ref, sorted_ref, new_hbm, change_hbm, ladder_hbm,
-    labels_ref, betas_ref, accept_ref, pairs_ref, new_ref, change_ref, ladder_ref,
-    field_ref, moment_ref, q0, m0, qa_0, qa_1, pa, qe_0, qe_1, pe, perm, perm_back,
-    got_0, got_1, got_2, picked_0, picked_1, picked_2, label_row, label_tab, act_row, act_got, act_sum, act_tab, holder_row, holder_ref,
-    send_h, recv_h, send_1, recv_1, send_2, recv_2, send_lab, recv_lab, send_act, recv_act, local_sem, load_sem, small_sem, store_sem,
+    out_ref, sorted_ref, label_out, act_out,
+    labels_ref, betas_ref, accept_ref, pairs_ref,
+    field_ref, moment_ref, q0, m0, qm_0, qm_1, pm, qa_0, qa_1, pa, qe_0, qe_1, pe, perm, perm_back,
+    got_0, got_1, got_2, got_3, picked_0, picked_1, picked_2, picked_3, label_row, label_tab, act_row, act_got, act_sum, act_tab, holder_row, holder_ref,
+    send_h, recv_h, send_1, recv_1, send_2, recv_2, send_lab, recv_lab, send_act, recv_act, local_sem, load_sem, small_sem,
 ):
     me = lax.axis_index("rep")
     dom = lax.axis_index("dom")
@@ -83,8 +81,10 @@
     x, z, y, c = split_rep(me)
     place = table_place(me)
     group = lax.div(place, 8)
-    got = (got_0, got_1, got_2)
-    picked = (picked_0, picked_1, picked_2)
+    got = (got_0, got_1, got_2, got_3)
+    picked = (picked_0, picked_1, picked_2, picked_3)
+    part_of_me, lane_of_me = lax.div(me, 16), lax.rem(me, 16)
+    turned = [lax.rem(lane_of_me + k, 16) for k in range(16)]
 
     loads = []
     for first, n in ((32, 64), (0, 32), (96, 32)):
@@ -120,9 +120,7 @@
     coldness = betas_ref[label]
     new_label = pairs_ref[label]
     accepted = accept_ref[0] == 1
-    new_ref[0] = new_label
-    stores = [pltpu.make_async_copy(new_ref, new_hbm, store_sem.at[0])]
-    stores[0].start()
+    label_out[...] = jnp.full((1, 128), new_label, jnp.int32)
     label_row[...] = jnp.full((1, 128), new_label, jnp.int32)
 
     i0 = lax.broadcasted_iota(jnp.int32, (256, 256), 0)
@@ -161,17 +159,17 @@
             new = jnp.where(accepted, values[at : at + n], field_ref[pl.ds(first, n), :])
             out_ref[pl.ds(first // 8, n // 8)] = new.reshape(n // 8, 8, 2048)
 
-    def set_apart(first, stride):
+    def set_apart(first, count):
         def one(n, carry):
-            apart(field_ref, q0, first + stride * n)
-            apart(moment_ref, m0, first + stride * n)
+            apart(field_ref, q0, first + n)
+            apart(moment_ref, m0, first + n)
             return carry
 
-        lax.fori_loop(0, 2, one, 0)
+        lax.fori_loop(0, count, one, 0)
 
     loads[0].wait()
     loads[1].wait()
-    set_apart(1, 1)
+    set_apart(1, 2)
 
     row = lax.broadcasted_iota(jnp.int32, (8, 2048), 0)
     a = coldness * (EPS * HOP)
@@ -207,30 +205,26 @@
         change = (0.5 * moment * moment + coldness * new) - (0.5 * start * start + coldness * old)
         return sums[0] + fold(change), sums[1] + fold(jnp.where(accepted, new, old))
 
-    def inner(base, count):
-        def sweep(src, dst, mom, first):
-            def some(n, carry):
-                for k in range(6):
-                    at = base + 8 * n + k
-                    leap(src, at, mom, at, dst, pa, at, first)
-                return carry
-
-            lax.fori_loop(0, count, some, 0)
+    def inner(even, odd, mom, base):
+        def sweep(src, dst, src_p, first):
+            for at in range(base, base + 6):
+                leap(src, at, src_p, at, dst, mom, at, first)
 
         def pair(n, carry):
-            sweep(qa_0, qa_1, pa, False)
-            sweep(qa_1, qa_0, pa, False)
+            sweep(even, odd, mom, False)
+            sweep(odd, even, mom, False)
             return carry
 
-        sweep(q0, qa_0, m0, True)
+        sweep(q0, even, m0, True)
         lax.fori_loop(0, 3, pair, 0)
-        sweep(qa_0, qa_1, pa, False)
-
-    def inner_last(first, last, sums):
-        return lax.fori_loop(first, last, lambda i, sums: finish(qa_1, i, pa, i, i, sums), sums)
-
-    inner(7, 1)
-    settle(joined(qa_1[pl.ds(64, 32), :]), [(0, 32, 48)])
+        sweep(even, odd, mom, False)
+        first = 8 * base - 8
+        settle(joined(odd[pl.ds(16 + first, 32), :]), [(0, 32, first)])
+
+    def inner_last(odd, mom, first, sums):
+        return lax.fori_loop(first, first + 4, lambda i, sums: finish(odd, i, mom, i, i, sums), sums)
+
+    inner(qm_0, qm_1, pm, 7)
 
     def to_column(src, tab, send_sem, recv_sem):
         for k in range(8):
@@ -244,13 +238,24 @@
                 join_rep((x + k // 4) % 4, z, (y + (k // 2) % 2) % 2, (c + k % 2) % 2),
             )
 
-    def spread(chunk, first=0, last=128):
-        def one(k, carry):
-            home = lax.rem(me + k, 128)
-            push(tile_of(out_ref, chunk, home), got[chunk].at[me], send_1.at[chunk], recv_1.at[chunk], home)
+    def each(start, finish_part=None):
+        def one(n, carry):
+            part = lax.rem(part_of_me + n, 8)
+            for k in range(16):
+                start(part, turned[k], part * 16 + turned[k])
+                if finish_part is not None and k % 4 == 3:
+                    finish_part(n, k // 4)
             return carry
 
-        lax.fori_loop(first, last, one, 0, unroll=4)
+        lax.fori_loop(0, 8, one, 0)
+
+    def spread(chunk, beside=None):
+        mine = got[chunk].at[me]
+
+        def start(part, at, home):
+            push(half_tile(out_ref, chunk, part, at), mine, send_1.at[chunk], recv_1.at[chunk], home)
+
+        each(start, beside)
 
     def pick(chunk):
         def one(t, carry):
@@ -260,17 +265,17 @@
         lax.fori_loop(0, 128, one, 0, unroll=8)
 
     def give(chunk):
-        def one(k, carry):
-            goal = lax.rem(me + k, 128)
-            push(picked[chunk].at[goal], tile_of(sorted_ref, chunk, me), send_2.at[chunk], recv_2, goal)
-            return carry
-
-        lax.fori_loop(0, 128, one, 0, unroll=4)
+        mine = half_tile(sorted_ref, chunk, part_of_me, lane_of_me)
+
+        def start(part, at, goal):
+            push(picked[chunk].at[goal], mine, send_2.at[chunk], recv_2, goal)
+
+        each(start)
 
     halos = ((q0, 136, 8), (q0, 16, 144), (m0, 136, 8), (m0, 16, 144))
     edges = ((q0, 135, 7), (q0, 24, 152))
 
-    def halo(k, n):
+    def halo(n, k):
         ref, src_row, dst_row = halos[k]
         cols = pl.ds(pl.multiple_of(256 * n, 128), 256)
         push(
@@ -281,29 +286,22 @@
     pl.semaphore_wait(barrier, 128)
     to_column(label_row, label_tab.at[0], send_lab.at[0], recv_lab.at[0])
     spread(0)
-    zero = jnp.zeros((8, 128), F32)
-    sums = inner_last(8, 12, (zero, zero))
-    for load in loads[2:]:
-        load.wait()
-    set_apart(0, 3)
+
+    loads[2].wait()
+    loads[3].wait()
+    set_apart(0, 1)
+    inner(qa_0, qa_1, pa, 3)
     wait_for(label_tab.at[0, pl.ds(0, 8)], recv_lab.at[0])
     to_plane(label_tab.at[0], label_tab.at[1], send_lab.at[1], recv_lab.at[1])
-    inner(3, 2)
-    for part in range(2):
-        settle(joined(qa_1[pl.ds(32 + 64 * part, 32), :]), [(0, 32, 16 + 64 * part)])
-
+    spread(1)
+
+    loads[4].wait()
+    loads[5].wait()
+    set_apart(3, 1)
+    inner(qa_0, qa_1, pa, 11)
     for k, (ref, src_row, dst_row) in enumerate(edges):
         push(ref.at[pl.ds(src_row, 1)], ref.at[pl.ds(dst_row, 1)], send_h.at[4 + k], recv_h.at[4 + k], me)
-
-    def spread_and_halo(n, carry):
-        for k in range(4):
-            halo(k, n)
-            for at in range(4):
-                home = lax.rem(me + 16 * n + 4 * k + at, 128)
-                push(tile_of(out_ref, 1, home), got_1.at[me], send_1.at[1], recv_1.at[1], home)
-        return carry
-
-    lax.fori_loop(0, 8, spread_and_halo, 0)
+    spread(2, halo)
 
     lane = lax.broadcasted_iota(jnp.int32, (1, 128), 1)
     wait_for(label_tab.at[1], recv_lab.at[1])
@@ -319,8 +317,9 @@
     wait_for(got_0, recv_1.at[0])
     pick(0)
     give(0)
-    sums = inner_last(4, 8, sums)
-    sums = inner_last(12, 16, sums)
+    wait_for(got_1, recv_1.at[1])
+    pick(1)
+    give(1)
 
     for k, (ref, src_row, dst_row) in enumerate(halos):
         wait_for(ref.at[pl.ds(dst_row, 8)], recv_h.at[k])
@@ -348,28 +347,32 @@
         joined(jnp.concatenate((qe_1[pl.ds(16, 16), :], qe_1[pl.ds(64, 16), :]), 0)),
         [(0, 16, 0), (16, 16, 112)],
     )
-    spread(2)
+    spread(3)
 
     def outer_last(i, sums):
         side, local = lax.div(i, 2), 2 + lax.rem(i, 2)
         return finish(qe_1, 6 * side + local, pe, 6 * side + local, 14 * side + local, sums)
 
-    sums = lax.fori_loop(0, 4, outer_last, sums)
+    zero = jnp.zeros((8, 128), F32)
+    sums = lax.fori_loop(0, 4, outer_last, (zero, zero))
+    sums = inner_last(qm_1, pm, 8, sums)
+    sums = inner_last(qa_1, pa, 4, sums)
+    sums = inner_last(qa_1, pa, 12, sums)
     act_row[...] = jnp.where(lane == 0, jnp.sum(sums[1]), jnp.where(lane == 1, jnp.sum(sums[0]), 0.0))
     push(act_row, act_got, send_act.at[0], recv_act.at[0], me)
 
-    wait_for(got_1, recv_1.at[1])
-    pick(1)
-    give(1)
+    wait_for(got_2, recv_1.at[2])
+    pick(2)
+    give(2)
     wait_for(act_got, recv_act.at[0])
     total = act_row[...] + act_got[...]
     act_sum[...] = total
     to_column(act_sum, act_tab.at[0], send_act.at[1], recv_act.at[1])
-    wait_for(got_2, recv_1.at[2])
-    pick(2)
+    wait_for(got_3, recv_1.at[3])
+    pick(3)
     wait_for(act_tab.at[0, pl.ds(0, 8)], recv_act.at[1])
     to_plane(act_tab.at[0], act_tab.at[1], send_act.at[2], recv_act.at[2])
-    give(2)
+    give(3)
 
     for k, (ref, src_row, dst_row) in enumerate(halos):
         wait_for(ref.at[pl.ds(src_row, 8)], send_h.at[k])
@@ -379,31 +382,30 @@
     wait_for(label_tab.at[1], send_lab.at[1])
     wait_for(act_got, send_act.at[0])
     wait_for(act_tab.at[0, pl.ds(0, 8)], send_act.at[1])
-    for chunk in range(3):
+    for chunk in range(CHUNKS):
         wait_for(got[chunk], send_1.at[chunk])
-    change_ref[0] = jnp.sum(jnp.where(lane == 1, total, 0.0))
-    stores.append(pltpu.make_async_copy(change_ref, change_hbm, store_sem.at[1]))
-    stores[1].start()
     wait_for(act_tab.at[1], recv_act.at[2])
     ladder = jnp.zeros((1, 128), F32)
     for p in range(128):
         ladder = ladder + jnp.where(label_tab[1, p] == me, act_tab[1, p], 0.0)
-    ladder_ref[0] = jnp.sum(jnp.where(lane == 0, ladder, 0.0)) / 524288.0
-    stores.append(pltpu.make_async_copy(ladder_ref, ladder_hbm, store_sem.at[2]))
-    stores[2].start()
-    for copy in stores:
-        copy.wait()
+    act_out[...] = jnp.where(lane == 0, ladder / 524288.0, total)
     wait_for(act_tab.at[1], send_act.at[2])
-    for chunk in range(3):
+    for chunk in range(CHUNKS):
         wait_for(got[chunk], send_2.at[chunk])
     wait_for(sorted_ref, recv_2)
 
 
-def hand_over(out_in, sorted_in, new_in, change_in, ladder_in, out, ordered, new, change, ladder, sems):
-    pairs = ((out_in, out), (sorted_in, ordered), (new_in, new), (change_in, change), (ladder_in, ladder))
-    copies = [pltpu.make_async_copy(src, dst, sems.at[k]) for k, (src, dst) in enumerate(pairs)]
+def hand_over(out_in, sorted_in, label_in, act_in, out, ordered, new, change, ladder, new_s, change_s, ladder_s, sems):
+    copies = [pltpu.make_async_copy(out_in, out, sems.at[0]), pltpu.make_async_copy(sorted_in, ordered, sems.at[1])]
     for copy in copies:
         copy.start()
+    lane = lax.broadcasted_iota(jnp.int32, (1, 128), 1)
+    new_s[0] = jnp.max(label_in[...])
+    change_s[0] = jnp.sum(jnp.where(lane == 1, act_in[...], 0.0))
+    ladder_s[0] = jnp.sum(jnp.where(lane == 0, act_in[...], 0.0))
+    for k, (src, dst) in enumerate(((new_s, new), (change_s, change), (ladder_s, ladder))):
+        copies.append(pltpu.make_async_copy(src, dst, sems.at[2 + k]))
+        copies[-1].start()
     for copy in copies:
         copy.wait()
 
@@ -418,21 +420,22 @@
         strip, strip, jax.ShapeDtypeStruct((1,), i32),
         jax.ShapeDtypeStruct((1,), F32), jax.ShapeDtypeStruct((1,), F32),
     )
+    smalls = (jax.ShapeDtypeStruct((1, 128), i32), jax.ShapeDtypeStruct((1, 128), F32))
     results = pl.pallas_call(
         whole,
-        out_shape=shapes,
+        out_shape=(strip, strip, *smalls),
         in_specs=[hbm] * 6,
-        out_specs=(vmem, vmem, hbm, hbm, hbm),
+        out_specs=(vmem,) * 4,
         scratch_shapes=[
             pltpu.SMEM((1,), i32),
             pltpu.SMEM((128,), F32),
             pltpu.SMEM((1,), i32),
             pltpu.SMEM((128,), i32),
-            pltpu.SMEM((1,), i32),
-            pltpu.SMEM((1,), F32),
-            pltpu.SMEM((1,), F32),
             pltpu.VMEM((128, 2048), F32),
             pltpu.VMEM((128, 2048), F32),
+            pltpu.VMEM((160, 2048), F32),
+            pltpu.VMEM((160, 2048), F32),
+            pltpu.VMEM((160, 2048), F32),
             pltpu.VMEM((160, 2048), F32),
             pltpu.VMEM((160, 2048), F32),
             pltpu.VMEM((160, 2048), F32),
@@ -443,12 +446,7 @@
             pltpu.VMEM((96, 2048), F32),
             pltpu.VMEM((768, 256), BF16),
             pltpu.VMEM((512, 256), BF16),
-            pltpu.VMEM((128, 4, 128), F32),
-            pltpu.VMEM((128, 8, 128), F32),
-            pltpu.VMEM((128, 4, 128), F32),
-            pltpu.VMEM((128, 4, 128), F32),
-            pltpu.VMEM((128, 8, 128), F32),
-            pltpu.VMEM((128, 4, 128), F32),
+            *[pltpu.VMEM((128, 4, 128), F32)] * 8,
             pltpu.VMEM((1, 128), i32),
             pltpu.VMEM((2, 128, 1, 128), i32),
             pltpu.VMEM((1, 128), F32),
@@ -457,17 +455,17 @@
             pltpu.VMEM((2, 128, 1, 128), F32),
             pltpu.VMEM((1, 128), i32),
             pltpu.SMEM((1, 128), i32),
-            dma((6,)), dma((6,)), dma((3,)), dma((3,)), dma((3,)), dma(()),
-            dma((2,)), dma((2,)), dma((3,)), dma((3,)), dma(()), dma((6,)), dma((4,)), dma((3,)),
+            dma((6,)), dma((6,)), dma((4,)), dma((4,)), dma((4,)), dma(()),
+            dma((2,)), dma((2,)), dma((3,)), dma((3,)), dma(()), dma((6,)), dma((4,)),
         ],
         compiler_params=pltpu.CompilerParams(collective_id=0, has_side_effects=True, vmem_limit_bytes=53_500_000),
     )(field, momentum, labels, betas, accept, swap_pairs)
     out, ordered, new_label, change, ladder = pl.pallas_call(
         hand_over,
         out_shape=shapes,
-        in_specs=[vmem, vmem, hbm, hbm, hbm],
+        in_specs=[vmem] * 4,
         out_specs=(hbm,) * 5,
-        scratch_shapes=[dma((5,))],
+        scratch_shapes=[pltpu.SMEM((1,), i32), pltpu.SMEM((1,), F32), pltpu.SMEM((1,), F32), dma((5,))],
         compiler_params=pltpu.CompilerParams(vmem_limit_bytes=8 << 20),
     )(*results)
     return out.reshape(1, 128, 2048), ordered.reshape(1, 128, 2048), new_label, change, ladder

time: 72.8 us -> 70.2 us (0.964)
  Pallas kernels: 70.6 us -> 68.1 us
    pallas_call x2, Pallas kernels: 70.6 us -> 68.1 us  [the longest x1 66.7 us: body(): pl.pallas_call(whole, out_shape=(strip, strip, *smalls), in_specs=[hbm] *...]
where the time goes in v5:
time: 70.2 us; the launch traced here: 70.1 us
  Pallas kernels  68.1 us (97%)
  between operations  1.98 us (3%)
    pallas_call x1, Pallas kernels, body(): pl.pallas_call(whole, out_shape=(strip, strip, *smalls), in_specs=[hbm] *...  66.7 us

profile of v5, /device:TPU:1, one launch (start us, length us, event | category | flops | bytes accessed | tf_op | source)
XLA Modules:
  0.0 70.1 jit_solution(8032329167322937880)
XLA Ops:
  1.3 0.0 copy-start
  1.3 0.0 copy-start.1
  2.0 0.0 copy-done
  2.0 0.0 copy-done.1
  2.0 66.7 %shard_map.101 = (f32[16,8,2048]{2,1,0:T(8,128)S(1)}, f32[16,8,2048]{2,1,0:T(8,128)S(1)}, s32[1,128]{1,0:T(1,128)S(1)}, f32[1,128]{1,0:T(1,128)S(1)}) custom-call(f32[1,128,2048]{2,1,0:T(8,128)} %field_hbm.1, f32[1,128,2048]{2,1,0:T(8,128)} %moment_hbm.1, s32[1]{0:T(128)S(6)} %copy.11.labels_hbm, f32[128]{0:T(128)S(1)} %copy-done, s32[1]{0:T(128)S(6)} %copy.12.accept_hbm, ...), custom_call_target="tpu_custom_call" | custom-call | tf_op jit(solution)/shard_map/pallas_call | solution.py:424
  68.7 1.4 %shard_map.102 = (f32[16,8,2048]{2,1,0:T(8,128)}, f32[16,8,2048]{2,1,0:T(8,128)}, s32[1]{0:T(128)}, f32[1]{0:T(128)}, f32[1]{0:T(128)}) custom-call(f32[16,8,2048]{2,1,0:T(8,128)S(1)} %get-tuple-element.14.out_in, f32[16,8,2048]{2,1,0:T(8,128)S(1)} %get-tuple-element.15.sorted_in, s32[1,128]{1,0:T(1,128)S(1)} %get-tuple-element.16.label_in, ...), custom_call_target="tpu_custom_call" | custom-call | tf_op jit(solution)/shard_map/pallas_call | solution.py:463
Async XLA Ops:
  1.3 0.7 copy-start
  1.3 0.7 copy-start.1

commit v6 on v5

--- a/solution.py
+++ b/solution.py
@@ -317,6 +317,10 @@
     wait_for(got_0, recv_1.at[0])
     pick(0)
     give(0)
+    zero = jnp.zeros((8, 128), F32)
+    sums = inner_last(qm_1, pm, 8, (zero, zero))
+    sums = inner_last(qa_1, pa, 4, sums)
+    sums = inner_last(qa_1, pa, 12, sums)
     wait_for(got_1, recv_1.at[1])
     pick(1)
     give(1)
@@ -353,11 +357,7 @@
         side, local = lax.div(i, 2), 2 + lax.rem(i, 2)
         return finish(qe_1, 6 * side + local, pe, 6 * side + local, 14 * side + local, sums)
 
-    zero = jnp.zeros((8, 128), F32)
-    sums = lax.fori_loop(0, 4, outer_last, (zero, zero))
-    sums = inner_last(qm_1, pm, 8, sums)
-    sums = inner_last(qa_1, pa, 4, sums)
-    sums = inner_last(qa_1, pa, 12, sums)
+    sums = lax.fori_loop(0, 4, outer_last, sums)
     act_row[...] = jnp.where(lane == 0, jnp.sum(sums[1]), jnp.where(lane == 1, jnp.sum(sums[0]), 0.0))
     push(act_row, act_got, send_act.at[0], recv_act.at[0], me)
 

time: 70.2 us -> 70.2 us (level)
  no operation moved by 1% of the time
where the time goes in v6:
time: 70.2 us; the launch traced here: 70.1 us
  Pallas kernels  68.1 us (97%)
  between operations  1.98 us (3%)
    pallas_call x1, Pallas kernels, body(): pl.pallas_call(whole, out_shape=(strip, strip, *smalls), in_specs=[hbm] *...  66.7 us

profile of v6, /device:TPU:1, one launch (start us, length us, event | category | flops | bytes accessed | tf_op | source)
XLA Modules:
  0.0 70.1 jit_solution(9439398874444075957)
XLA Ops:
  1.3 0.0 copy-start
  1.3 0.0 copy-start.1
  2.0 0.0 copy-done
  2.0 0.0 copy-done.1
  2.0 66.7 %shard_map.101 = (f32[16,8,2048]{2,1,0:T(8,128)S(1)}, f32[16,8,2048]{2,1,0:T(8,128)S(1)}, s32[1,128]{1,0:T(1,128)S(1)}, f32[1,128]{1,0:T(1,128)S(1)}) custom-call(f32[1,128,2048]{2,1,0:T(8,128)} %field_hbm.1, f32[1,128,2048]{2,1,0:T(8,128)} %moment_hbm.1, s32[1]{0:T(128)S(6)} %copy.11.labels_hbm, f32[128]{0:T(128)S(1)} %copy-done, s32[1]{0:T(128)S(6)} %copy.12.accept_hbm, ...), custom_call_target="tpu_custom_call" | custom-call | tf_op jit(solution)/shard_map/pallas_call | solution.py:424
  68.7 1.4 %shard_map.102 = (f32[16,8,2048]{2,1,0:T(8,128)}, f32[16,8,2048]{2,1,0:T(8,128)}, s32[1]{0:T(128)}, f32[1]{0:T(128)}, f32[1]{0:T(128)}) custom-call(f32[16,8,2048]{2,1,0:T(8,128)S(1)} %get-tuple-element.14.out_in, f32[16,8,2048]{2,1,0:T(8,128)S(1)} %get-tuple-element.15.sorted_in, s32[1,128]{1,0:T(1,128)S(1)} %get-tuple-element.16.label_in, ...), custom_call_target="tpu_custom_call" | custom-call | tf_op jit(solution)/shard_map/pallas_call | solution.py:463
Async XLA Ops:
  1.3 0.7 copy-start
  1.3 0.7 copy-start.1
